TPU v7x, 32 devices: a whole 2x2x4 slice. The times are simulated.
32 devices in a mesh: ep: 32 (over z, y, x, core).
Axes of the slice: x: 2, y: 2, z: 4, core: 2. Of those that a mesh axis runs over, the one named last changes fastest.
Arguments:
- x_tokens: bfloat16 [131072, 768], P('ep')
- w_router: float32 [768, 32], replicated
- expert_idx: int32 [131072], P('ep')
- w_in: bfloat16 [32, 768, 3072], P('ep')
- w_out: bfloat16 [32, 3072, 768], P('ep')
- grad_y: bfloat16 [131072, 768], P('ep')
Outputs:
- output 1: bfloat16 [131072, 768], P('ep')
- output 2: float32 [32, 768, 3072], P('ep')
- output 3: float32 [32, 3072, 768], P('ep')
- output 4: float32 [768, 32], replicated
- output 5: float32 [], replicated
- output 6: float32 [], replicated
All inputs are finite; a program needn't handle non-finite values.
Results may differ from a plain program's by a relative error of at most 0.012471.
Values are sent between devices in bfloat16 or wider.
A program may use at most 1 GiB of HBM per device.

v0:
```python
import jax
import jax.numpy as jnp
from jax import lax
from jax.sharding import PartitionSpec as P

AUX_WEIGHT = 0.01
Z_WEIGHT = 0.001
CHUNKS = 2
BLOCK = 256
BF = jnp.bfloat16
F32 = jnp.float32


def route(idx, num_experts, capacity):
    tokens = idx.shape[0]
    hot = (idx[:, None] == jnp.arange(num_experts, dtype=jnp.int32)[None, :]).astype(BF)
    blocks = hot.reshape(tokens // BLOCK, BLOCK, num_experts)
    row = lax.broadcasted_iota(jnp.int32, (BLOCK, BLOCK), 0)
    col = lax.broadcasted_iota(jnp.int32, (BLOCK, BLOCK), 1)
    inside = jnp.einsum('ij,bje->bie', (col <= row).astype(BF), blocks, preferred_element_type=F32)
    totals = inside[:, -1, :]
    n_blocks = tokens // BLOCK
    earlier = (jnp.arange(n_blocks)[None, :] < jnp.arange(n_blocks)[:, None]).astype(F32)
    before = jnp.sum(earlier[:, :, None] * totals[None, :, :], axis=1)
    counts = (before[-1] + totals[-1]).astype(jnp.int32)
    position = jnp.sum((inside + before[:, None, :]) * blocks.astype(F32), axis=-1).reshape(tokens).astype(jnp.int32) - 1
    pos_hot = (position[:, None] == jnp.arange(capacity, dtype=jnp.int32)[None, :]).astype(BF)
    token = jnp.arange(tokens, dtype=jnp.int32)
    parts = jnp.concatenate([hot * (token // 64).astype(BF)[:, None], hot * (token % 64).astype(BF)[:, None]], axis=1)
    found = jnp.einsum('te,tp->ep', parts, pos_hot, preferred_element_type=F32)
    slot_tok = (64.0 * found[:num_experts] + found[num_experts:]).astype(jnp.int32)
    return hot, pos_hot, counts, position, slot_tok


def rows_of(source, index):
    return source.at[index].get(mode='promise_in_bounds')


def router(rows, w_router):
    logits = jnp.dot(rows, w_router, preferred_element_type=F32)
    return jax.nn.softmax(logits, axis=-1), jax.nn.logsumexp(logits, axis=-1)


def solution(mesh):
    n_dev = mesh.shape['ep']

    def expert_layer(x_tokens, w_router, expert_idx, w_in, w_out, grad_y):
        tokens, d_model = x_tokens.shape
        num_experts = n_dev
        capacity = (5 * tokens + 4 * num_experts - 1) // (4 * num_experts)
        total_tok = tokens * n_dev
        width = capacity // CHUNKS
        me = lax.axis_index('ep')
        w_in, w_out = w_in[0], w_out[0]

        def exchange(rows):
            return lax.all_to_all(rows, 'ep', 0, 0, tiled=True)

        hot, pos_hot, counts, position, slot_tok = route(expert_idx, num_experts, capacity)
        hot_f = hot.astype(F32)
        all_counts = exchange(jnp.broadcast_to(counts[None, :], (n_dev, num_experts)))

        n_rows = n_dev * width
        first = slot_tok[:, :width]
        second = slot_tok[:, width:]

        def picked(source, index):
            return rows_of(source, index.reshape(-1)).reshape(n_dev, index.shape[1], d_model)

        x_first, all_counts = lax.optimization_barrier((picked(x_tokens, first), all_counts))
        x_first = exchange(x_first).reshape(n_rows, d_model)
        arriving = lax.dynamic_index_in_dim(all_counts, me, 1, keepdims=False)
        load_frac = jnp.sum(all_counts, axis=0).astype(F32) / total_tok
        dy_first, x_first = lax.optimization_barrier((picked(grad_y, first), x_first))
        dy_first = exchange(dy_first).reshape(n_rows, d_model)
        x_last, dy_first = lax.optimization_barrier((picked(x_tokens, second), dy_first))
        x_last = exchange(x_last).reshape(n_rows, d_model)
        dy_last, x_last = lax.optimization_barrier((picked(grad_y, second), x_last))
        dy_last = exchange(dy_last).reshape(n_rows, d_model)

        prob, log_norm = router(x_tokens, w_router)
        gate = jnp.sum(prob * hot_f, axis=-1)
        aux_vec = AUX_WEIGHT * num_experts * load_frac / total_tok
        spread = jnp.sum(prob * aux_vec, axis=-1, keepdims=True)
        d_logits = prob * (aux_vec - spread) + (2.0 * Z_WEIGHT / total_tok * log_norm)[:, None] * prob
        part_router = jnp.einsum('sd,se->de', x_tokens, d_logits, preferred_element_type=F32)

        mine = (jnp.arange(num_experts) == me).astype(F32)[None, :]

        def forward(j, rows, dy):
            slot_prob, _ = router(rows, w_router)
            slot_gate = jnp.sum(slot_prob * mine, axis=-1)
            hidden = jnp.maximum(jnp.dot(rows, w_in, preferred_element_type=F32), 0.0).astype(BF)
            expert_out = jnp.dot(hidden, w_out, preferred_element_type=F32).astype(BF)
            dy_f = dy.astype(F32)
            slots = j * width + jnp.arange(width, dtype=jnp.int32)
            valid = (slots[None, :] < arriving[:, None]).reshape(n_rows)
            slot_dot = jnp.where(valid, jnp.sum(expert_out.astype(F32) * dy_f, axis=-1), 0.0)
            scaled = jnp.where(valid[:, None], slot_gate[:, None] * dy_f, 0.0).astype(BF)
            slot_logits = (slot_gate * slot_dot)[:, None] * (mine - slot_prob)
            part = jnp.einsum('sd,se->de', rows, slot_logits, preferred_element_type=F32)
            return hidden, scaled, slot_dot.reshape(n_dev, width), part

        def backward(hidden, scaled):
            d_hidden = jnp.einsum('nd,fd->nf', scaled, w_out, preferred_element_type=F32)
            d_pre = jnp.where(hidden > 0, d_hidden, 0.0).astype(BF)
            d_rows = jnp.einsum('nf,df->nd', d_pre, w_in, preferred_element_type=F32).astype(BF)
            return d_pre, d_rows.reshape(n_dev, width, d_model)

        def weights(rows, hidden, scaled, d_pre):
            return (jnp.einsum('nd,nf->df', rows, d_pre, preferred_element_type=F32),
                    jnp.einsum('nf,nd->fd', hidden, scaled, preferred_element_type=F32))

        hidden_a, scaled_a, dot_a, part_a = forward(0, x_first, dy_first)
        pre_a, d_rows_a = backward(hidden_a, scaled_a)
        in_a, out_a = weights(x_first, hidden_a, scaled_a, pre_a)
        d_rows_a, in_a, out_a = lax.optimization_barrier((d_rows_a, in_a, out_a))
        back_a = exchange(d_rows_a)
        hidden_b, scaled_b, dot_b, part_b = forward(1, x_last, dy_last)
        pre_b, d_rows_b = backward(hidden_b, scaled_b)

        part_router += part_a + part_b
        slices = part_router.reshape(n_dev, -1)
        prob_sum = jnp.sum(prob, axis=0)[:, None]
        z_sum = jnp.full((n_dev, 1), jnp.sum(log_norm * log_norm))
        payload = jnp.concatenate([dot_a, dot_b, slices, prob_sum, z_sum], axis=1)
        payload, back_a, d_rows_b = lax.optimization_barrier((payload, back_a, d_rows_b))
        payload = exchange(payload)
        payload, d_rows_b = lax.optimization_barrier((payload, d_rows_b))
        back_b = exchange(d_rows_b)
        reduced = jnp.sum(payload[:, capacity:], axis=0)
        reduced, back_b = lax.optimization_barrier((reduced, back_b))
        totals = exchange(jnp.broadcast_to(reduced[None, :], (n_dev, reduced.shape[0])))
        grad_w_router = totals[:, :-2].reshape(d_model, num_experts)
        aux_loss = AUX_WEIGHT * num_experts * jnp.sum(load_frac * (totals[:, -2] / total_tok))
        z_loss = Z_WEIGHT * totals[0, -1] / total_tok

        payload, hidden_b, pre_b, back_a = lax.optimization_barrier((payload, hidden_b, pre_b, back_a))
        in_b, out_b = weights(x_last, hidden_b, scaled_b, pre_b)

        all_dot = payload[:, :capacity]
        spread_dot = jnp.dot(hot_f, all_dot, precision=lax.Precision.HIGHEST, preferred_element_type=F32)
        d_gate = jnp.sum(jnp.where(pos_hot > 0, spread_dot, 0.0), axis=-1)
        d_logits += (gate * d_gate)[:, None] * (hot_f - prob)
        dx = jnp.einsum('se,de->sd', d_logits, w_router)
        for j, back in enumerate((back_a, back_b)):
            inside = position - j * width
            index = expert_idx * width + jnp.clip(inside, 0, width - 1)
            held = (inside >= 0) & (inside < width)
            dx += jnp.where(held[:, None], rows_of(back.reshape(n_rows, d_model), index).astype(F32), 0.0)
        return dx.astype(BF), (in_a + in_b)[None], (out_a + out_b)[None], grad_w_router, aux_loss, z_loss

    return jax.shard_map(expert_layer, mesh=mesh,
                         in_specs=(P('ep', None), P(None, None), P('ep'), P('ep', None, None), P('ep', None, None), P('ep', None)),
                         out_specs=(P('ep', None), P('ep', None, None), P('ep', None, None), P(None, None), P(), P()),
                         check_vma=False)
```

profile of v0, /device:TPU:3, one launch (start us, length us, event | category | flops | bytes accessed | tf_op | source)
XLA Modules:
  0.0 676.0 jit_solution(15705925584979719370)
XLA Ops:
  0.7 0.8 eq.51
  1.4 0.3 convolution_bitcast_fusion
  1.7 0.3 slice_reduce_fusion
  2.3 0.6 broadcast_in_dim.72
  2.9 6.4 all-to-all-start
  9.3 0.2 multiply_reduce_fusion.2
  9.5 0.6 clamp_bitcast_fusion
  10.2 0.8 fusion.36
  11.0 0.6 fusion.18
  11.8 13.9 %gather_fusion = bf16[2560,768]{1,0:T(8,128)(2,1)} fusion(bf16[4096,768]{1,0:T(8,128)(2,1)} %param.6, s32[3072]{0:T(1024)S(1)} %pad_clamp_fusion.1), kind=kCustom, calls=%fused_computation | custom fusion | bytes 7874560 | tf_op jit(solution)/shard_map/gather | solution.py:36
  25.7 5.9 all-to-all-start.1
  31.6 13.9 %gather_fusion.1 = bf16[2560,768]{1,0:T(8,128)(2,1)} fusion(bf16[4096,768]{1,0:T(8,128)(2,1)} %param.11, s32[3072]{0:T(1024)S(1)} %pad_clamp_fusion.1), kind=kCustom, calls=%fused_computation.1 | custom fusion | bytes 7874560 | tf_op jit(solution)/shard_map/gather | solution.py:36
  45.5 73.3 %all-to-all-done.1 = bf16[32,80,768]{2,1,0:T(8,128)(2,1)} async-done(((bf16[32,80,768]{2,1,0:T(8,128)(2,1)}), bf16[32,80,768]{2,1,0:T(8,128)(2,1)}, u32[]{:S(2)}, u32[]{:S(2)}) %all-to-all-start.1) | async-done | bytes 3932192 | tf_op jit(solution)/shard_map/all_to_all | solution.py:57
  118.9 5.1 all-to-all-start.2
  124.1 13.9 %gather_fusion.2 = bf16[2560,768]{1,0:T(8,128)(2,1)} fusion(bf16[4096,768]{1,0:T(8,128)(2,1)} %param.6, s32[3072]{0:T(1024)S(1)} %pad_clamp_fusion), kind=kCustom, calls=%fused_computation.2 | custom fusion | bytes 7874560 | tf_op jit(solution)/shard_map/gather | solution.py:36
  138.0 73.2 %all-to-all-done.2 = bf16[32,80,768]{2,1,0:T(8,128)(2,1)} async-done(((bf16[32,80,768]{2,1,0:T(8,128)(2,1)}), bf16[32,80,768]{2,1,0:T(8,128)(2,1)}, u32[]{:S(2)}, u32[]{:S(2)}) %all-to-all-start.2) | async-done | bytes 3932192 | tf_op jit(solution)/shard_map/all_to_all | solution.py:57
  211.2 5.8 all-to-all-start.3
  217.0 13.9 %gather_fusion.3 = bf16[2560,768]{1,0:T(8,128)(2,1)} fusion(bf16[4096,768]{1,0:T(8,128)(2,1)} %param.11, s32[3072]{0:T(1024)S(1)} %pad_clamp_fusion), kind=kCustom, calls=%fused_computation.3 | custom fusion | bytes 7874560 | tf_op jit(solution)/shard_map/gather | solution.py:36
  230.9 4.7 fusion.96
  235.8 0.2 dynamic-slice_reduce_fusion
  236.1 0.4 copy-done.22
  236.6 0.7 lt.135
  237.3 1.0 fusion.26
  238.3 0.7 copy.39
  239.0 1.2 multiply_reduce_fusion.6
  240.2 3.4 fusion.95
  243.7 18.7 %maximum_convert_fusion.1 = bf16[2560,3072]{1,0:T(8,128)(2,1)} fusion(bf16[2560,768]{1,0:T(8,128)(2,1)} %bitcast.6, bf16[1,768,3072]{2,1,0:T(8,128)(2,1)} %param.9), kind=kOutput, calls=%fused_computation.9 | convolution fusion | flops 12095324160 | bytes 24379392 | tf_op jit(solution)/shard_map/dot_general | solution.py:93
  262.4 6.3 copy.36
  268.7 18.1 %fusion = f32[2560]{0:T(1024)S(1)} fusion(bf16[2560,768]{0,1:T(8,128)(2,1)} %copy.36, bf16[2560,3072]{1,0:T(8,128)(2,1)} %maximum_convert_fusion.1, bf16[1,3072,768]{2,1,0:T(8,128)(2,1)} %param.10), kind=kOutput, calls=%fused_computation.15 | convolution fusion | flops 12089423872 | bytes 24389632 | tf_op jit(solution)/shard_map/dot_general | solution.py:94
  286.9 17.2 %all-to-all-done.3 = bf16[32,80,768]{2,1,0:T(8,128)(2,1)} async-done(((bf16[32,80,768]{2,1,0:T(8,128)(2,1)}), bf16[32,80,768]{2,1,0:T(8,128)(2,1)}, u32[]{:S(2)}, u32[]{:S(2)}) %all-to-all-start.3) | async-done | bytes 3932192 | tf_op jit(solution)/shard_map/all_to_all | solution.py:57
  304.1 3.5 fusion.94
  307.7 0.2 multiply_reduce_fusion.3
  307.9 19.0 %select_convert_fusion.1 = bf16[2560,3072]{1,0:T(8,128)(2,1)} fusion(bf16[2560,3072]{1,0:T(8,128)(2,1)} %maximum_convert_fusion.1, bf16[1,3072,768]{2,1,0:T(8,128)(2,1)} %param.10, bf16[2560,768]{0,1:T(8,128)(2,1)S(1)} %copy-done.3, f32[2560]{0:T(1024)S(1)} %get-tuple-element.79, pred[2560]{0:T(1024)(128)(4,1)S(1)} %lt.134), kind=kOutput, calls=%fused_computation.7 | convolution fusion | flops 12111052800 | bytes 40120832 | tf_op jit(solution)/shard_map/nd,fd->nf/dot_general | solution.py:105
  326.9 17.5 %fusion.14 = f32[3072,768]{1,0:T(8,128)} fusion(bf16[2560,3072]{1,0:T(8,128)(2,1)} %maximum_convert_fusion.1, bf16[2560,768]{0,1:T(8,128)(2,1)S(1)} %copy-done.3, f32[2560]{0:T(1024)S(1)} %get-tuple-element.79, pred[2560]{0:T(1024)(128)(4,1)S(1)} %lt.134), kind=kOutput, calls=%fused_computation.37 | convolution fusion | flops 12087459840 | bytes 29110784 | tf_op jit(solution)/shard_map/nf,nd->fd/dot_general | solution.py:112
  344.4 5.1 all-to-all-start.4
  349.4 18.3 %fusion.97 = f32[768,3072]{1,0:T(8,128)} fusion(bf16[2560,768]{1,0:T(8,128)(2,1)} %bitcast.6, bf16[2560,3072]{1,0:T(8,128)(2,1)} %select_convert_fusion.1), kind=kOutput, calls=%fused_computation.166 | convolution fusion | flops 12079595520 | bytes 29097984 | tf_op jit(solution)/shard_map/nd,nf->df/dot_general | solution.py:111
  367.7 17.8 %convolution_convert_fusion.1 = bf16[2560,768]{1,0:T(8,128)(2,1)} fusion(bf16[2560,3072]{1,0:T(8,128)(2,1)} %select_convert_fusion.1, bf16[1,768,3072]{2,1,0:T(8,128)(2,1)} %param.9), kind=kOutput, calls=%fused_computation.22 | convolution fusion | flops 12081561600 | bytes 24379392 | tf_op jit(solution)/shard_map/nf,df->nd/dot_general | solution.py:107
  385.6 2.9 fusion.42
  388.6 18.9 %maximum_convert_fusion = bf16[2560,3072]{1,0:T(8,128)(2,1)} fusion(bf16[2560,768]{1,0:T(8,128)(2,1)} %bitcast.12, bf16[1,768,3072]{2,1,0:T(8,128)(2,1)} %param.9), kind=kOutput, calls=%fused_computation.8 | convolution fusion | flops 12095324160 | bytes 24379392 | tf_op jit(solution)/shard_map/dot_general | solution.py:93
  407.5 29.2 %all-to-all-done.4 = bf16[32,80,768]{2,1,0:T(8,128)(2,1)} async-done(((bf16[32,80,768]{2,1,0:T(8,128)(2,1)}), bf16[32,80,768]{2,1,0:T(8,128)(2,1)}, u32[]{:S(2)}, u32[]{:S(2)}) %all-to-all-start.4) | async-done | bytes 3932192 | tf_op jit(solution)/shard_map/all_to_all | solution.py:57
  436.7 5.1 all-to-all-start.5
  441.8 6.7 copy.37
  448.5 18.5 %multiply_reduce_fusion = f32[2560]{0:T(1024)S(1)} fusion(f32[2560,768]{0,1:T(8,128)} %copy.37, bf16[2560,3072]{1,0:T(8,128)(2,1)} %maximum_convert_fusion, bf16[1,3072,768]{2,1,0:T(8,128)(2,1)} %param.10), kind=kOutput, calls=%fused_computation.20 | convolution fusion | flops 12087457792 | bytes 28321792 | tf_op jit(solution)/shard_map/dot_general | solution.py:94
  467.2 2.9 convolution_add_fusion
  470.1 4.0 fusion.25
  474.6 0.6 broadcast_in_dim.129
  475.3 4.0 select_convert_fusion.3
  479.4 21.5 %select_convert_fusion = bf16[2560,3072]{1,0:T(8,128)(2,1)} fusion(bf16[2560,3072]{1,0:T(8,128)(2,1)} %maximum_convert_fusion, bf16[2560,768]{1,0:T(8,128)(2,1)} %bitcast.96, bf16[1,3072,768]{2,1,0:T(8,128)(2,1)} %param.10), kind=kOutput, calls=%fused_computation.6 | convolution fusion | flops 12103188480 | bytes 40108032 | tf_op jit(solution)/shard_map/nd,fd->nf/dot_general | solution.py:105
  500.9 17.8 %convolution_convert_fusion = bf16[2560,768]{1,0:T(8,128)(2,1)} fusion(bf16[2560,3072]{1,0:T(8,128)(2,1)} %select_convert_fusion, bf16[1,768,3072]{2,1,0:T(8,128)(2,1)} %param.9), kind=kOutput, calls=%fused_computation.21 | convolution fusion | flops 12081561600 | bytes 24379392 | tf_op jit(solution)/shard_map/nf,df->nd/dot_general | solution.py:107
  518.7 10.3 %all-to-all-done.5 = bf16[32,80,768]{2,1,0:T(8,128)(2,1)} async-done(((bf16[32,80,768]{2,1,0:T(8,128)(2,1)}), bf16[32,80,768]{2,1,0:T(8,128)(2,1)}, u32[]{:S(2)}, u32[]{:S(2)}) %all-to-all-start.5) | async-done | bytes 3932192 | tf_op jit(solution)/shard_map/all_to_all | solution.py:57
  529.1 11.7 %all_to_all.60 = f32[32,1,930]{2,1,0:T(1,128)S(1)} all-to-all(f32[32,1,930]{2,1,0:T(1,128)S(1)} %copy.40), channel_id=1, replica_groups=mesh['ep'=32] {'ep'}, dimensions={0} | all-to-all | bytes 238080 | tf_op jit(solution)/shard_map/all_to_all | solution.py:57
  540.9 5.3 all-to-all-start.7
  546.3 21.7 %gather_fusion.4 = bf16[4096,768]{1,0:T(8,128)(2,1)} fusion(bf16[2560,768]{1,0:T(8,128)(2,1)} %bitcast.20, s32[4096]{0:T(1024)S(1)} %get-tuple-element.84), kind=kCustom, calls=%fused_computation.4 | custom fusion | bytes 12599296 | tf_op jit(solution)/shard_map/gather | solution.py:36
  568.1 1.6 fusion.23
  569.8 20.6 %add_bitcast_fusion.1 = f32[1,768,3072]{2,1,0:T(8,128)} fusion(f32[768,3072]{1,0:T(8,128)} %fusion.97, bf16[2560,768]{1,0:T(8,128)(2,1)} %bitcast.12, bf16[2560,3072]{1,0:T(8,128)(2,1)} %select_convert_fusion), kind=kOutput, calls=%fused_computation.14 | convolution fusion | flops 12081954816 | bytes 38535168 | tf_op jit(solution)/shard_map/nd,nf->df/dot_general | solution.py:111
  590.5 22.0 %add_bitcast_fusion = f32[1,3072,768]{2,1,0:T(8,128)} fusion(f32[3072,768]{1,0:T(8,128)} %fusion.14, bf16[2560,3072]{1,0:T(8,128)(2,1)} %maximum_convert_fusion, f32[2560,768]{0,1:T(8,128)} %copy.37, f32[2560]{0:T(1024)S(1)} %get-tuple-element.78, pred[2560]{0:T(1024)(128)(4,1)S(1)} %copy-done.21), kind=kOutput, calls=%fused_computation.13 | convolution fusion | flops 12087853056 | bytes 42480128 | tf_op jit(solution)/shard_map/nf,nd->fd/dot_general | solution.py:112
  612.4 21.0 %all-to-all-done.7 = bf16[32,80,768]{2,1,0:T(8,128)(2,1)} async-done(((bf16[32,80,768]{2,1,0:T(8,128)(2,1)}), bf16[32,80,768]{2,1,0:T(8,128)(2,1)}, u32[]{:S(2)}, u32[]{:S(2)}) %all-to-all-start.7) | async-done | bytes 3932192 | tf_op jit(solution)/shard_map/all_to_all | solution.py:57
  633.4 0.7 broadcast_in_dim.143
  634.1 5.0 all-to-all-start.8
  639.1 21.7 %gather_fusion.5 = bf16[4096,768]{1,0:T(8,128)(2,1)} fusion(bf16[2560,768]{1,0:T(8,128)(2,1)} %bitcast.21, s32[4096]{0:T(1024)S(1)} %get-tuple-element.85), kind=kCustom, calls=%fused_computation.5 | custom fusion | bytes 12599296 | tf_op jit(solution)/shard_map/gather | solution.py:36
  660.8 9.2 %add_convert_fusion = bf16[4096,768]{1,0:T(8,128)(2,1)} fusion(bf16[4096,768]{1,0:T(8,128)(2,1)} %gather_fusion.5, bf16[4096,768]{1,0:T(8,128)(2,1)} %gather_fusion.4, f32[768,32]{0,1:T(8,128)S(1)} %copy-done, pred[4096]{0:T(1024)(128)(4,1)S(1)} %and.47, pred[4096]{0:T(1024)(128)(4,1)S(1)} %compare_and_fusion.1, f32[4096]{0:T(1024)S(1)} %mul.209, ...), kind=kOutput, calls=%fused_computation.10 | convolution fusion | flops 224788480 | bytes 19603584 | tf_op jit(solution)/shard_map/se,de->sd/dot_general | solution.py:145
  670.1 0.7 slice.71
  670.9 0.8 copy.42
  671.7 0.6 multiply_reduce_fusion.7
  (107 shorter events, 2.6 us)
Async XLA Ops:
  0.6 230.3 %copy-start = (f32[768,32]{0,1:T(8,128)S(1)}, f32[768,32]{0,1:T(8,128)}, u32[]{:S(2)}) copy-start(f32[768,32]{0,1:T(8,128)} %param.7) | copy-start | bytes 294916
  2.9 22.8 %all-to-all-start = ((s32[32,1,32]{2,1,0:T(1,128)}), s32[32,1,32]{2,1,0:T(1,128)S(1)}, u32[]{:S(2)}, u32[]{:S(2)}) async-start(s32[32,1,32]{2,1,0:T(1,128)} %broadcast_in_dim.72), calls=%async_computation | async-start | bytes 32768 | tf_op jit(solution)/shard_map/all_to_all | solution.py:57
  9.5 0.7 copy-start.10
  10.2 1.4 copy-start.12
  25.7 93.1 %all-to-all-start.1 = ((bf16[32,80,768]{2,1,0:T(8,128)(2,1)}), bf16[32,80,768]{2,1,0:T(8,128)(2,1)}, u32[]{:S(2)}, u32[]{:S(2)}) async-start(bf16[32,80,768]{2,1,0:T(8,128)(2,1)} %bitcast.95), calls=%async_computation.1 | async-start | bytes 7864320 | tf_op jit(solution)/shard_map/all_to_all | solution.py:57
  118.9 92.3 %all-to-all-start.2 = ((bf16[32,80,768]{2,1,0:T(8,128)(2,1)}), bf16[32,80,768]{2,1,0:T(8,128)(2,1)}, u32[]{:S(2)}, u32[]{:S(2)}) async-start(bf16[32,80,768]{2,1,0:T(8,128)(2,1)} %bitcast.94), calls=%async_computation.2 | async-start | bytes 7864320 | tf_op jit(solution)/shard_map/all_to_all | solution.py:57
  211.2 92.9 %all-to-all-start.3 = ((bf16[32,80,768]{2,1,0:T(8,128)(2,1)}), bf16[32,80,768]{2,1,0:T(8,128)(2,1)}, u32[]{:S(2)}, u32[]{:S(2)}) async-start(bf16[32,80,768]{2,1,0:T(8,128)(2,1)} %bitcast.93), calls=%async_computation.3 | async-start | bytes 7864320 | tf_op jit(solution)/shard_map/all_to_all | solution.py:57
  230.9 6.4 copy-start.6
  230.9 5.7 copy-start.26
  235.6 26.8 %copy-start.1 = (f32[4096,32]{0,1:T(8,128)}, f32[4096,32]{0,1:T(8,128)S(1)}, u32[]{:S(2)}) copy-start(f32[4096,32]{0,1:T(8,128)S(1)} %get-tuple-element.99) | copy-start | bytes 1572868
  235.7 26.8 %copy-start.4 = (f32[4096]{0:T(1024)}, f32[4096]{0:T(1024)S(1)}, u32[]{:S(2)}) copy-start(f32[4096]{0:T(1024)S(1)} %get-tuple-element.98) | copy-start | bytes 49156
  235.8 26.6 %copy-start.8 = (f32[4096]{0:T(1024)}, f32[4096]{0:T(1024)S(1)}, u32[]{:S(2)}) copy-start(f32[4096]{0:T(1024)S(1)} %fusion.38) | copy-start | bytes 49156
  235.8 26.6 %copy-start.28 = (s32[32]{0:T(128)}, s32[32]{0:T(128)S(1)}, u32[]{:S(2)}) copy-start(s32[32]{0:T(128)S(1)} %reduce_sum.169) | copy-start | bytes 388
  236.0 0.5 copy-start.22
  236.5 0.8 copy-start.19
  237.3 25.1 %copy-start.24 = (f32[32]{0:T(128)}, f32[32]{0:T(128)S(1)}, u32[]{:S(2)}) copy-start(f32[32]{0:T(128)S(1)} %convert_multiply_fusion.3) | copy-start | bytes 388
  304.1 3.8 copy-start.3
  344.4 92.3 %all-to-all-start.4 = ((bf16[32,80,768]{2,1,0:T(8,128)(2,1)}), bf16[32,80,768]{2,1,0:T(8,128)(2,1)}, u32[]{:S(2)}, u32[]{:S(2)}) async-start(bf16[32,80,768]{2,1,0:T(8,128)(2,1)} %bitcast.92), calls=%async_computation.4 | async-start | bytes 7864320 | tf_op jit(solution)/shard_map/all_to_all | solution.py:57
  436.7 92.3 %all-to-all-start.5 = ((bf16[32,80,768]{2,1,0:T(8,128)(2,1)}), bf16[32,80,768]{2,1,0:T(8,128)(2,1)}, u32[]{:S(2)}, u32[]{:S(2)}) async-start(bf16[32,80,768]{2,1,0:T(8,128)(2,1)} %bitcast.97), calls=%async_computation.5 | async-start | bytes 7864320 | tf_op jit(solution)/shard_map/all_to_all | solution.py:57
  448.5 18.6 %copy-start.21 = (pred[2560]{0:T(1024)(128)(4,1)S(1)}, pred[2560]{0:T(1024)(128)(4,1)}, u32[]{:S(2)}) copy-start(pred[2560]{0:T(1024)(128)(4,1)} %lt.135) | copy-start | bytes 7684
  448.5 21.6 %copy-start.2 = (f32[4096,32]{0,1:T(8,128)S(1)}, f32[4096,32]{0,1:T(8,128)}, u32[]{:S(2)}) copy-start(f32[4096,32]{0,1:T(8,128)} %copy-done.1) | copy-start | bytes 1572868
  448.5 21.6 %copy-start.5 = (f32[4096]{0:T(1024)S(1)}, f32[4096]{0:T(1024)}, u32[]{:S(2)}) copy-start(f32[4096]{0:T(1024)} %copy-done.4) | copy-start | bytes 49156
  448.5 21.6 %copy-start.9 = (f32[4096]{0:T(1024)S(1)}, f32[4096]{0:T(1024)}, u32[]{:S(2)}) copy-start(f32[4096]{0:T(1024)} %copy-done.8) | copy-start | bytes 49156
  448.5 21.6 %copy-start.14 = (f32[4096]{0:T(1024)S(1)}, f32[4096]{0:T(1024)}, u32[]{:S(2)}) copy-start(f32[4096]{0:T(1024)} %get-tuple-element.76) | copy-start | bytes 49156
  448.5 21.6 %copy-start.15 = (f32[4096]{0:T(1024)S(1)}, f32[4096]{0:T(1024)}, u32[]{:S(2)}) copy-start(f32[4096]{0:T(1024)} %get-tuple-element.81) | copy-start | bytes 49156
  448.5 21.6 %copy-start.25 = (f32[32]{0:T(128)S(1)}, f32[32]{0:T(128)}, u32[]{:S(2)}) copy-start(f32[32]{0:T(128)} %copy-done.24) | copy-start | bytes 388
  467.1 7.4 %copy-start.23 = (s32[32]{0:T(128)S(1)}, s32[32]{0:T(128)}, u32[]{:S(2)}) copy-start(s32[32]{0:T(128)} %copy-done.22) | copy-start | bytes 388
  467.1 7.4 %copy-start.27 = (s32[80]{0:T(128)S(1)}, s32[80]{0:T(128)}, u32[]{:S(2)}) copy-start(s32[80]{0:T(128)} %copy-done.26) | copy-start | bytes 964
  467.1 8.1 %copy-start.18 = (f32[32,1]{1,0:T(8,128)S(1)}, f32[32,1]{1,0:T(8,128)}, u32[]{:S(2)}) copy-start(f32[32,1]{1,0:T(8,128)} %copy.39) | copy-start | bytes 388
  467.1 8.2 %copy-start.20 = (pred[32,80]{1,0:T(8,128)(4,1)S(1)}, pred[32,80]{1,0:T(8,128)(4,1)}, u32[]{:S(2)}) copy-start(pred[32,80]{1,0:T(8,128)(4,1)} %copy-done.19) | copy-start | bytes 7684
  518.7 27.5 %copy-start.17 = (s32[2,2,8,128]{3,2,1,0:T(8,128)S(1)}, s32[2,2,8,128]{3,2,1,0:T(8,128)}, u32[]{:S(2)}) copy-start(s32[2,2,8,128]{3,2,1,0:T(8,128)} %get-tuple-element.86) | copy-start | bytes 49156
  518.7 27.5 %copy-start.11 = (f32[16,256]{1,0:T(8,128)S(1)}, f32[16,256]{1,0:T(8,128)}, u32[]{:S(2)}) copy-start(f32[16,256]{1,0:T(8,128)} %copy-done.10) | copy-start | bytes 49156
  518.7 27.6 %copy-start.13 = (s32[2,2,8,128]{3,1,2,0:T(2,128)S(1)}, s32[2,2,8,128]{3,1,2,0:T(2,128)}, u32[]{:S(2)}) copy-start(s32[2,2,8,128]{3,1,2,0:T(2,128)} %copy-done.12) | copy-start | bytes 49156
  518.7 27.6 %copy-start.7 = (s32[4096]{0:T(1024)S(1)}, s32[4096]{0:T(1024)}, u32[]{:S(2)}) copy-start(s32[4096]{0:T(1024)} %param.8) | copy-start | bytes 49156
  540.9 92.5 %all-to-all-start.7 = ((bf16[32,80,768]{2,1,0:T(8,128)(2,1)}), bf16[32,80,768]{2,1,0:T(8,128)(2,1)}, u32[]{:S(2)}, u32[]{:S(2)}) async-start(bf16[32,80,768]{2,1,0:T(8,128)(2,1)} %bitcast.98), calls=%async_computation.7 | async-start | bytes 7864320 | tf_op jit(solution)/shard_map/all_to_all | solution.py:57
  546.3 23.4 %copy-start.16 = (f32[4096]{0:T(1024)S(1)}, f32[4096]{0:T(1024)}, u32[]{:S(2)}) copy-start(f32[4096]{0:T(1024)} %get-tuple-element.74) | copy-start | bytes 49156
  634.1 35.8 %all-to-all-start.8 = ((f32[32,1,770]{2,1,0:T(1,128)}), f32[32,1,770]{2,1,0:T(1,128)S(1)}, u32[]{:S(2)}, u32[]{:S(2)}) async-start(f32[32,1,770]{2,1,0:T(1,128)} %broadcast_in_dim.143), calls=%async_computation.8 | async-start | bytes 229376 | tf_op jit(solution)/shard_map/all_to_all | solution.py:57
  660.7 10.9 %copy-start.29 = (s32[32]{0:T(128)S(1)}, s32[32]{0:T(128)}, u32[]{:S(2)}) copy-start(s32[32]{0:T(128)} %copy-done.28) | copy-start | bytes 388
where the time goes:
time: 684 us; the launch traced here: 676 us
  matrix products  262 us (38%)
  waiting for transfers between devices  224 us (33%)
  local copies, waits for them, and re-layouts  120 us (18%)
  starting transfers between devices  43.6 us (6%)
  blocking collectives  11.7 us (2%)
  other arithmetic  9.58 us (1%)
    all_to_all x8, waiting for transfers between devices, exchange(): return lax.all_to_all(rows, 'ep', 0, 0, tiled=True)  224 us
    gather x6, local copies, waits for them, and re-layouts, rows_of(): return source.at[index].get(mode='promise_in_bounds')  99 us
    all_to_all x8, starting transfers between devices, exchange(): return lax.all_to_all(rows, 'ep', 0, 0, tiled=True)  43.6 us
    dot_general x2, matrix products, backward(): jnp.einsum('nd,fd->nf', scaled, w_out, preferred_element_type=F32)  40.5 us
    dot_general x2, matrix products, weights(): jnp.einsum('nf,nd->fd', hidden, scaled, preferred_element_type=F32)  39.5 us
    dot_general x2, matrix products, weights(): jnp.einsum('nd,nf->df', rows, d_pre, preferred_element_type=F32)  38.9 us
    dot_general x2, matrix products, forward(): jnp.dot(rows, w_in, preferred_element_type=F32)  37.6 us
    dot_general x2, matrix products, forward(): expert_out = jnp.dot(hidden, w_out, preferred_element_type=F32).astype(BF)  36.6 us
  transfers between devices with their start and end apart: 8, of which 6 were waited for; matrix products, arithmetic and copies ran while one was open for 51% of the time, Pallas kernels for 0%

commit v1 on v0

--- a/solution.py
+++ b/solution.py
@@ -113,8 +113,8 @@
 
         hidden_a, scaled_a, dot_a, part_a = forward(0, x_first, dy_first)
         pre_a, d_rows_a = backward(hidden_a, scaled_a)
-        in_a, out_a = weights(x_first, hidden_a, scaled_a, pre_a)
-        d_rows_a, in_a, out_a = lax.optimization_barrier((d_rows_a, in_a, out_a))
+        in_a = jnp.einsum('nd,nf->df', x_first, pre_a, preferred_element_type=F32)
+        d_rows_a, in_a = lax.optimization_barrier((d_rows_a, in_a))
         back_a = exchange(d_rows_a)
         hidden_b, scaled_b, dot_b, part_b = forward(1, x_last, dy_last)
         pre_b, d_rows_b = backward(hidden_b, scaled_b)
@@ -135,19 +135,25 @@
         aux_loss = AUX_WEIGHT * num_experts * jnp.sum(load_frac * (totals[:, -2] / total_tok))
         z_loss = Z_WEIGHT * totals[0, -1] / total_tok
 
-        payload, hidden_b, pre_b, back_a = lax.optimization_barrier((payload, hidden_b, pre_b, back_a))
+        payload, hidden_a, hidden_b, pre_b, back_a = lax.optimization_barrier((payload, hidden_a, hidden_b, pre_b, back_a))
+        out_a = jnp.einsum('nf,nd->fd', hidden_a, scaled_a, preferred_element_type=F32)
         in_b, out_b = weights(x_last, hidden_b, scaled_b, pre_b)
 
         all_dot = payload[:, :capacity]
+
+        def placed(j, back):
+            inside = position - j * width
+            index = jnp.where((inside >= 0) & (inside < width), expert_idx * width + inside, -1)
+            pick = (index[:, None] == jnp.arange(n_rows, dtype=jnp.int32)[None, :]).astype(BF)
+            return jnp.dot(pick, back.reshape(n_rows, d_model), preferred_element_type=F32)
+
         spread_dot = jnp.dot(hot_f, all_dot, precision=lax.Precision.HIGHEST, preferred_element_type=F32)
         d_gate = jnp.sum(jnp.where(pos_hot > 0, spread_dot, 0.0), axis=-1)
         d_logits += (gate * d_gate)[:, None] * (hot_f - prob)
         dx = jnp.einsum('se,de->sd', d_logits, w_router)
-        for j, back in enumerate((back_a, back_b)):
-            inside = position - j * width
-            index = expert_idx * width + jnp.clip(inside, 0, width - 1)
-            held = (inside >= 0) & (inside < width)
-            dx += jnp.where(held[:, None], rows_of(back.reshape(n_rows, d_model), index).astype(F32), 0.0)
+        dx += placed(0, back_a)
+        dx, back_b = lax.optimization_barrier((dx, back_b))
+        dx += placed(1, back_b)
         return dx.astype(BF), (in_a + in_b)[None], (out_a + out_b)[None], grad_w_router, aux_loss, z_loss
 
     return jax.shard_map(expert_layer, mesh=mesh,

time: 684 us -> 643 us (0.940)
  local copies, waits for them, and re-layouts: 120 us -> 77.2 us
  matrix products: 262 us -> 304 us
  waiting for transfers between devices: 224 us -> 189 us
  blocking collectives: 11.7 us -> 0 us
    dot_general x0 -> x4, matrix products: none -> 82.5 us  [the longest x2 45.9 us: placed(): jnp.dot(pick, back.reshape(n_rows, d_model), preferred_element_type=F32)]
    gather x6 -> x4, local copies, waits for them, and re-layouts: 99 us -> 55.6 us  [rows_of(): return source.at[index].get(mode='promise_in_bounds')]
    all_to_all x8 -> x9, waiting for transfers between devices: 224 us -> 189 us  [exchange(): return lax.all_to_all(rows, 'ep', 0, 0, tiled=True)]
    dot_general x2 -> x1, matrix products: 38.9 us -> 20.6 us  [weights(): jnp.einsum('nd,nf->df', rows, d_pre, preferred_element_type=F32)]
    dot_general x2 -> x1, matrix products: 39.5 us -> 22 us  [weights(): jnp.einsum('nf,nd->fd', hidden, scaled, preferred_element_type=F32)]
    all_to_all x1 -> x0, blocking collectives: 11.7 us -> none  [exchange(): return lax.all_to_all(rows, 'ep', 0, 0, tiled=True)]
    all_to_all x8 -> x9, starting transfers between devices: 43.6 us -> 49.9 us  [exchange(): return lax.all_to_all(rows, 'ep', 0, 0, tiled=True)]
  transfers between devices with their start and end apart: 8 -> 9, of which waited for: 6 -> 6; matrix products, arithmetic and copies ran while one was open for 51% -> 60% of each run, Pallas kernels for 0% -> 0%
where the time goes in v1:
time: 643 us; the launch traced here: 635 us
  matrix products  304 us (47%)
  waiting for transfers between devices  189 us (29%)
  local copies, waits for them, and re-layouts  77.2 us (12%)
  starting transfers between devices  49.9 us (8%)
  other arithmetic  9.54 us (1%)
    all_to_all x9, waiting for transfers between devices, exchange(): return lax.all_to_all(rows, 'ep', 0, 0, tiled=True)  189 us
    gather x4, local copies, waits for them, and re-layouts, rows_of(): return source.at[index].get(mode='promise_in_bounds')  55.6 us
    all_to_all x9, starting transfers between devices, exchange(): return lax.all_to_all(rows, 'ep', 0, 0, tiled=True)  49.9 us
    dot_general x2, matrix products, placed(): jnp.dot(pick, back.reshape(n_rows, d_model), preferred_element_type=F32)  45.9 us
    dot_general x2, matrix products, backward(): jnp.einsum('nd,fd->nf', scaled, w_out, preferred_element_type=F32)  40.6 us
    dot_general x2, matrix products, forward(): jnp.dot(rows, w_in, preferred_element_type=F32)  37.5 us
    dot_general x2, matrix products, forward(): expert_out = jnp.dot(hidden, w_out, preferred_element_type=F32).astype(BF)  36.6 us
    dot_general x2, matrix products, backward(): jnp.einsum('nf,df->nd', d_pre, w_in, preferred_element_type=F32).astype(BF)  33.7 us
  transfers between devices with their start and end apart: 9, of which 6 were waited for; matrix products, arithmetic and copies ran while one was open for 60% of the time, Pallas kernels for 0%

profile of v1, /device:TPU:3, one launch (start us, length us, event | category | flops | bytes accessed | tf_op | source)
XLA Modules:
  0.0 634.7 jit_solution(9056457593253405862)
XLA Ops:
  0.7 0.8 eq.77
  1.4 0.3 convolution_bitcast_fusion
  1.7 0.3 slice_reduce_fusion
  2.3 0.6 broadcast_in_dim.51
  2.9 6.4 %all-to-all-start = ((s32[32,1,32]{2,1,0:T(1,128)}), s32[32,1,32]{2,1,0:T(1,128)S(1)}, u32[]{:S(2)}, u32[]{:S(2)}) async-start(s32[32,1,32]{2,1,0:T(1,128)} %broadcast_in_dim.51), calls=%async_computation | async-start | bytes 32768 | tf_op jit(solution)/shard_map/all_to_all | solution.py:57
  9.3 0.2 multiply_reduce_fusion.2
  9.5 0.6 add_bitcast_fusion.2
  10.1 0.8 fusion.42
  10.9 0.6 fusion.23
  11.8 13.9 %gather_fusion = bf16[2560,768]{1,0:T(8,128)(2,1)} fusion(bf16[4096,768]{1,0:T(8,128)(2,1)} %param.6, s32[3072]{0:T(1024)S(1)} %pad_clamp_fusion.1), kind=kCustom, calls=%fused_computation | custom fusion | bytes 7874560 | tf_op jit(solution)/shard_map/gather | solution.py:36
  25.7 5.9 all-to-all-start.1
  31.6 13.9 %gather_fusion.1 = bf16[2560,768]{1,0:T(8,128)(2,1)} fusion(bf16[4096,768]{1,0:T(8,128)(2,1)} %param.11, s32[3072]{0:T(1024)S(1)} %pad_clamp_fusion.1), kind=kCustom, calls=%fused_computation.1 | custom fusion | bytes 7874560 | tf_op jit(solution)/shard_map/gather | solution.py:36
  45.5 73.3 %all-to-all-done.1 = bf16[32,80,768]{2,1,0:T(8,128)(2,1)} async-done(((bf16[32,80,768]{2,1,0:T(8,128)(2,1)}), bf16[32,80,768]{2,1,0:T(8,128)(2,1)}, u32[]{:S(2)}, u32[]{:S(2)}) %all-to-all-start.1) | async-done | bytes 3932192 | tf_op jit(solution)/shard_map/all_to_all | solution.py:57
  118.8 5.1 all-to-all-start.2
  124.1 13.9 %gather_fusion.2 = bf16[2560,768]{1,0:T(8,128)(2,1)} fusion(bf16[4096,768]{1,0:T(8,128)(2,1)} %param.6, s32[3072]{0:T(1024)S(1)} %pad_clamp_fusion), kind=kCustom, calls=%fused_computation.2 | custom fusion | bytes 7874560 | tf_op jit(solution)/shard_map/gather | solution.py:36
  138.0 73.2 %all-to-all-done.2 = bf16[32,80,768]{2,1,0:T(8,128)(2,1)} async-done(((bf16[32,80,768]{2,1,0:T(8,128)(2,1)}), bf16[32,80,768]{2,1,0:T(8,128)(2,1)}, u32[]{:S(2)}, u32[]{:S(2)}) %all-to-all-start.2) | async-done | bytes 3932192 | tf_op jit(solution)/shard_map/all_to_all | solution.py:57
  211.1 5.4 all-to-all-start.3
  216.6 13.9 %gather_fusion.3 = bf16[2560,768]{1,0:T(8,128)(2,1)} fusion(bf16[4096,768]{1,0:T(8,128)(2,1)} %param.11, s32[3072]{0:T(1024)S(1)} %pad_clamp_fusion), kind=kCustom, calls=%fused_computation.3 | custom fusion | bytes 7874560 | tf_op jit(solution)/shard_map/gather | solution.py:36
  230.5 4.7 fusion.98
  235.7 0.4 copy-done.22
  236.2 0.7 lt.120
  236.9 1.0 fusion.94
  237.9 0.7 copy.39
  238.6 1.2 multiply_reduce_fusion.6
  239.8 3.4 fusion.100
  243.3 18.7 %maximum_convert_fusion.1 = bf16[2560,3072]{1,0:T(8,128)(2,1)} fusion(bf16[2560,768]{1,0:T(8,128)(2,1)} %bitcast.6, bf16[1,768,3072]{2,1,0:T(8,128)(2,1)} %param.9), kind=kOutput, calls=%fused_computation.11 | convolution fusion | flops 12095324160 | bytes 24379392 | tf_op jit(solution)/shard_map/dot_general | solution.py:93
  262.1 6.3 copy.36
  268.3 18.1 %fusion.4 = f32[2560]{0:T(1024)S(1)} fusion(bf16[2560,768]{0,1:T(8,128)(2,1)} %copy.36, bf16[2560,3072]{1,0:T(8,128)(2,1)} %maximum_convert_fusion.1, bf16[1,3072,768]{2,1,0:T(8,128)(2,1)} %param.10), kind=kOutput, calls=%fused_computation.19 | convolution fusion | flops 12089423872 | bytes 24389632 | tf_op jit(solution)/shard_map/dot_general | solution.py:94
  286.6 17.1 %all-to-all-done.3 = bf16[32,80,768]{2,1,0:T(8,128)(2,1)} async-done(((bf16[32,80,768]{2,1,0:T(8,128)(2,1)}), bf16[32,80,768]{2,1,0:T(8,128)(2,1)}, u32[]{:S(2)}, u32[]{:S(2)}) %all-to-all-start.3) | async-done | bytes 3932192 | tf_op jit(solution)/shard_map/all_to_all | solution.py:57
  303.7 5.6 all-to-all-start.4
  309.3 3.5 fusion.99
  312.9 0.2 multiply_reduce_fusion.3
  313.1 19.0 %select_convert_fusion.1 = bf16[2560,3072]{1,0:T(8,128)(2,1)} fusion(bf16[2560,3072]{1,0:T(8,128)(2,1)} %maximum_convert_fusion.1, bf16[1,3072,768]{2,1,0:T(8,128)(2,1)} %param.10, bf16[2560,768]{0,1:T(8,128)(2,1)S(1)} %copy-done.3, f32[2560]{0:T(1024)S(1)} %get-tuple-element.83, pred[2560]{0:T(1024)(128)(4,1)S(1)} %lt.119), kind=kOutput, calls=%fused_computation.9 | convolution fusion | flops 12111052800 | bytes 40120832 | tf_op jit(solution)/shard_map/nd,fd->nf/dot_general | solution.py:105
  332.2 18.4 %fusion.101 = f32[768,3072]{1,0:T(8,128)} fusion(bf16[2560,768]{1,0:T(8,128)(2,1)} %bitcast.6, bf16[2560,3072]{1,0:T(8,128)(2,1)} %select_convert_fusion.1), kind=kOutput, calls=%fused_computation.167 | convolution fusion | flops 12079595520 | bytes 29097984 | tf_op jit(solution)/shard_map/nd,nf->df/dot_general | solution.py:116
  350.6 15.8 %convolution_convert_fusion.1 = bf16[2560,768]{1,0:T(8,128)(2,1)} fusion(bf16[2560,3072]{1,0:T(8,128)(2,1)S(1)} %copy-done.28, bf16[1,768,3072]{2,1,0:T(8,128)(2,1)} %param.9), kind=kOutput, calls=%fused_computation.27 | convolution fusion | flops 12081561600 | bytes 24379392 | tf_op jit(solution)/shard_map/nf,df->nd/dot_general | solution.py:107
  366.5 2.9 fusion.48
  369.4 18.7 %maximum_convert_fusion = bf16[2560,3072]{1,0:T(8,128)(2,1)} fusion(bf16[2560,768]{1,0:T(8,128)(2,1)} %bitcast.12, bf16[1,768,3072]{2,1,0:T(8,128)(2,1)} %param.9), kind=kOutput, calls=%fused_computation.10 | convolution fusion | flops 12095324160 | bytes 24379392 | tf_op jit(solution)/shard_map/dot_general | solution.py:93
  388.1 8.3 %all-to-all-done.4 = bf16[32,80,768]{2,1,0:T(8,128)(2,1)} async-done(((bf16[32,80,768]{2,1,0:T(8,128)(2,1)}), bf16[32,80,768]{2,1,0:T(8,128)(2,1)}, u32[]{:S(2)}, u32[]{:S(2)}) %all-to-all-start.4) | async-done | bytes 3932192 | tf_op jit(solution)/shard_map/all_to_all | solution.py:57
  396.4 5.1 all-to-all-start.5
  401.5 6.7 %copy.37 = f32[2560,768]{0,1:T(8,128)} copy(bf16[2560,768]{1,0:T(8,128)(2,1)} %bitcast.66) | data formatting | bytes 11796480 | tf_op jit(solution)/shard_map/convert_element_type | solution.py:95
  408.2 18.5 %multiply_reduce_fusion = f32[2560]{0:T(1024)S(1)} fusion(f32[2560,768]{0,1:T(8,128)} %copy.37, bf16[2560,3072]{1,0:T(8,128)(2,1)} %maximum_convert_fusion, bf16[1,3072,768]{2,1,0:T(8,128)(2,1)} %param.10), kind=kOutput, calls=%fused_computation.24 | convolution fusion | flops 12087457792 | bytes 28321792 | tf_op jit(solution)/shard_map/dot_general | solution.py:94
  426.9 2.9 convolution_add_fusion
  429.9 4.0 fusion.30
  434.3 0.6 broadcast_in_dim.56
  435.1 4.0 select_convert_fusion.3
  439.1 21.6 %select_convert_fusion = bf16[2560,3072]{1,0:T(8,128)(2,1)} fusion(bf16[2560,3072]{1,0:T(8,128)(2,1)} %maximum_convert_fusion, bf16[2560,768]{1,0:T(8,128)(2,1)} %bitcast.98, bf16[1,3072,768]{2,1,0:T(8,128)(2,1)} %param.10), kind=kOutput, calls=%fused_computation.8 | convolution fusion | flops 12103188480 | bytes 40108032 | tf_op jit(solution)/shard_map/nd,fd->nf/dot_general | solution.py:105
  460.7 17.9 %convolution_convert_fusion = bf16[2560,768]{1,0:T(8,128)(2,1)} fusion(bf16[2560,3072]{1,0:T(8,128)(2,1)} %select_convert_fusion, bf16[1,768,3072]{2,1,0:T(8,128)(2,1)} %param.9), kind=kOutput, calls=%fused_computation.26 | convolution fusion | flops 12081561600 | bytes 24379392 | tf_op jit(solution)/shard_map/nf,df->nd/dot_general | solution.py:107
  478.5 10.2 %all-to-all-done.5 = bf16[32,80,768]{2,1,0:T(8,128)(2,1)} async-done(((bf16[32,80,768]{2,1,0:T(8,128)(2,1)}), bf16[32,80,768]{2,1,0:T(8,128)(2,1)}, u32[]{:S(2)}, u32[]{:S(2)}) %all-to-all-start.5) | async-done | bytes 3932192 | tf_op jit(solution)/shard_map/all_to_all | solution.py:57
  488.7 0.8 copy.40
  489.5 5.0 all-to-all-start.6
  494.6 6.8 %all-to-all-done.6 = f32[32,1,930]{2,1,0:T(1,128)S(1)} async-done(((f32[32,1,930]{2,1,0:T(1,128)}), f32[32,1,930]{2,1,0:T(1,128)S(1)}, u32[]{:S(2)}, u32[]{:S(2)}) %all-to-all-start.6) | async-done | bytes 119072 | tf_op jit(solution)/shard_map/all_to_all | solution.py:57
  501.5 1.6 fusion.28
  503.2 5.1 all-to-all-start.7
  508.3 18.2 %fusion.19 = f32[3072,768]{1,0:T(8,128)} fusion(bf16[2560,3072]{1,0:T(8,128)(2,1)} %maximum_convert_fusion.1, bf16[2560,768]{0,1:T(8,128)(2,1)} %copy.36, f32[2560]{0:T(1024)S(1)} %get-tuple-element.83, pred[2560]{0:T(1024)(128)(4,1)S(1)} %lt.119), kind=kOutput, calls=%fused_computation.42 | convolution fusion | flops 12087459840 | bytes 29110784 | tf_op jit(solution)/shard_map/nf,nd->fd/dot_general | solution.py:139
  526.5 20.6 %add_bitcast_fusion.1 = f32[1,768,3072]{2,1,0:T(8,128)} fusion(f32[768,3072]{1,0:T(8,128)} %fusion.101, bf16[2560,768]{1,0:T(8,128)(2,1)} %bitcast.12, bf16[2560,3072]{1,0:T(8,128)(2,1)} %select_convert_fusion), kind=kOutput, calls=%fused_computation.18 | convolution fusion | flops 12081954816 | bytes 38535168 | tf_op jit(solution)/shard_map/nd,nf->df/dot_general | solution.py:111
  547.0 6.5 %fusion.34 = f32[4096,768]{1,0:T(8,128)} fusion(f32[768,32]{0,1:T(8,128)S(1)} %copy-done, f32[4096]{0:T(1024)S(1)} %mul.209, f32[4096]{0:T(1024)S(1)} %copy-done.11, f32[4096]{0:T(1024)S(1)} %copy-done.10, f32[32]{0:T(128)S(1)} %copy-done.21, s32[4096]{0:T(1024)S(1)} %copy-done.7, f32[4096,32]{0,1:T(8,128)S(1)} %copy-done.2, f32[4096]{0:T(1024)S(1)} %copy-done.9, ...), kind=kOutput, calls=%fused_computation.57 | convolution fusion | flops 202768384 | bytes 13303936 | tf_op jit(solution)/shard_map/se,de->sd/dot_general | solution.py:153
  553.5 22.0 %add_bitcast_fusion = f32[1,3072,768]{2,1,0:T(8,128)} fusion(f32[3072,768]{1,0:T(8,128)} %fusion.19, bf16[2560,3072]{1,0:T(8,128)(2,1)} %maximum_convert_fusion, f32[2560,768]{0,1:T(8,128)} %copy.37, f32[2560]{0:T(1024)S(1)} %get-tuple-element.82, pred[2560]{0:T(1024)(128)(4,1)S(1)} %copy-done.19), kind=kOutput, calls=%fused_computation.17 | convolution fusion | flops 12087853056 | bytes 42480128 | tf_op jit(solution)/shard_map/nf,nd->fd/dot_general | solution.py:112
  575.5 23.2 %fusion.7 = f32[4096,768]{1,0:T(8,128)} fusion(f32[4096,768]{1,0:T(8,128)} %fusion.34, bf16[2560,768]{1,0:T(8,128)(2,1)} %bitcast.20, s32[4096]{0:T(1024)S(1)} %get-tuple-element.89), kind=kOutput, calls=%fused_computation.25 | convolution fusion | flops 16119758848 | bytes 29114368 | tf_op jit(solution)/shard_map/dot_general | solution.py:148
  598.7 0.7 broadcast_in_dim.67
  599.4 6.3 all-to-all-start.8
  605.7 22.8 %add_convert_fusion = bf16[4096,768]{1,0:T(8,128)(2,1)} fusion(f32[4096,768]{1,0:T(8,128)} %fusion.7, bf16[2560,768]{1,0:T(8,128)(2,1)} %bitcast.21, s32[4096]{0:T(1024)S(1)} %get-tuple-element.88), kind=kOutput, calls=%fused_computation.14 | convolution fusion | flops 16122904576 | bytes 22822912 | tf_op jit(solution)/shard_map/dot_general | solution.py:148
  628.6 0.7 slice.67
  629.5 0.8 copy.42
  630.3 0.6 multiply_reduce_fusion.7
  (103 shorter events, 2.6 us)
Async XLA Ops:
  0.6 229.9 %copy-start = (f32[768,32]{0,1:T(8,128)S(1)}, f32[768,32]{0,1:T(8,128)}, u32[]{:S(2)}) copy-start(f32[768,32]{0,1:T(8,128)} %param.7) | copy-start | bytes 294916
  2.9 22.8 %all-to-all-start = ((s32[32,1,32]{2,1,0:T(1,128)}), s32[32,1,32]{2,1,0:T(1,128)S(1)}, u32[]{:S(2)}, u32[]{:S(2)}) async-start(s32[32,1,32]{2,1,0:T(1,128)} %broadcast_in_dim.51), calls=%async_computation | async-start | bytes 32768 | tf_op jit(solution)/shard_map/all_to_all | solution.py:57
  10.1 1.5 copy-start.13
  25.7 93.1 %all-to-all-start.1 = ((bf16[32,80,768]{2,1,0:T(8,128)(2,1)}), bf16[32,80,768]{2,1,0:T(8,128)(2,1)}, u32[]{:S(2)}, u32[]{:S(2)}) async-start(bf16[32,80,768]{2,1,0:T(8,128)(2,1)} %bitcast.97), calls=%async_computation.1 | async-start | bytes 7864320 | tf_op jit(solution)/shard_map/all_to_all | solution.py:57
  118.8 92.3 %all-to-all-start.2 = ((bf16[32,80,768]{2,1,0:T(8,128)(2,1)}), bf16[32,80,768]{2,1,0:T(8,128)(2,1)}, u32[]{:S(2)}, u32[]{:S(2)}) async-start(bf16[32,80,768]{2,1,0:T(8,128)(2,1)} %bitcast.96), calls=%async_computation.2 | async-start | bytes 7864320 | tf_op jit(solution)/shard_map/all_to_all | solution.py:57
  211.1 92.5 %all-to-all-start.3 = ((bf16[32,80,768]{2,1,0:T(8,128)(2,1)}), bf16[32,80,768]{2,1,0:T(8,128)(2,1)}, u32[]{:S(2)}, u32[]{:S(2)}) async-start(bf16[32,80,768]{2,1,0:T(8,128)(2,1)} %bitcast.95), calls=%async_computation.3 | async-start | bytes 7864320 | tf_op jit(solution)/shard_map/all_to_all | solution.py:57
  230.5 6.4 %copy-start.6 = (s32[4096]{0:T(1024)S(1)}, s32[4096]{0:T(1024)}, u32[]{:S(2)}) copy-start(s32[4096]{0:T(1024)} %param.8) | copy-start | bytes 49156
  230.5 5.7 copy-start.24
  235.3 26.8 %copy-start.1 = (f32[4096,32]{0,1:T(8,128)}, f32[4096,32]{0,1:T(8,128)S(1)}, u32[]{:S(2)}) copy-start(f32[4096,32]{0,1:T(8,128)S(1)} %get-tuple-element.99) | copy-start | bytes 1572868
  235.3 26.8 %copy-start.4 = (f32[4096]{0:T(1024)}, f32[4096]{0:T(1024)S(1)}, u32[]{:S(2)}) copy-start(f32[4096]{0:T(1024)S(1)} %get-tuple-element.98) | copy-start | bytes 49156
  235.4 26.6 %copy-start.8 = (f32[4096]{0:T(1024)}, f32[4096]{0:T(1024)S(1)}, u32[]{:S(2)}) copy-start(f32[4096]{0:T(1024)S(1)} %fusion.44) | copy-start | bytes 49156
  235.4 26.6 %copy-start.26 = (s32[32]{0:T(128)}, s32[32]{0:T(128)S(1)}, u32[]{:S(2)}) copy-start(s32[32]{0:T(128)S(1)} %reduce_sum.169) | copy-start | bytes 388
  235.6 0.5 copy-start.22
  236.1 0.8 copy-start.17
  236.9 25.1 %copy-start.20 = (f32[32]{0:T(128)}, f32[32]{0:T(128)S(1)}, u32[]{:S(2)}) copy-start(f32[32]{0:T(128)S(1)} %convert_multiply_fusion.3) | copy-start | bytes 388
  303.7 92.7 %all-to-all-start.4 = ((bf16[32,80,768]{2,1,0:T(8,128)(2,1)}), bf16[32,80,768]{2,1,0:T(8,128)(2,1)}, u32[]{:S(2)}, u32[]{:S(2)}) async-start(bf16[32,80,768]{2,1,0:T(8,128)(2,1)} %bitcast.94), calls=%async_computation.4 | async-start | bytes 7864320 | tf_op jit(solution)/shard_map/all_to_all | solution.py:57
  309.3 3.8 copy-start.3
  332.2 18.4 %copy-start.28 = (bf16[2560,3072]{1,0:T(8,128)(2,1)S(1)}, bf16[2560,3072]{1,0:T(8,128)(2,1)}, u32[]{:S(2)}) copy-start(bf16[2560,3072]{1,0:T(8,128)(2,1)} %select_convert_fusion.1) | copy-start | bytes 47185924
  396.4 92.3 %all-to-all-start.5 = ((bf16[32,80,768]{2,1,0:T(8,128)(2,1)}), bf16[32,80,768]{2,1,0:T(8,128)(2,1)}, u32[]{:S(2)}, u32[]{:S(2)}) async-start(bf16[32,80,768]{2,1,0:T(8,128)(2,1)} %bitcast.100), calls=%async_computation.5 | async-start | bytes 7864320 | tf_op jit(solution)/shard_map/all_to_all | solution.py:57
  408.2 18.6 %copy-start.19 = (pred[2560]{0:T(1024)(128)(4,1)S(1)}, pred[2560]{0:T(1024)(128)(4,1)}, u32[]{:S(2)}) copy-start(pred[2560]{0:T(1024)(128)(4,1)} %lt.120) | copy-start | bytes 7684
  408.2 21.6 %copy-start.2 = (f32[4096,32]{0,1:T(8,128)S(1)}, f32[4096,32]{0,1:T(8,128)}, u32[]{:S(2)}) copy-start(f32[4096,32]{0,1:T(8,128)} %copy-done.1) | copy-start | bytes 1572868
  408.2 21.6 %copy-start.5 = (f32[4096]{0:T(1024)S(1)}, f32[4096]{0:T(1024)}, u32[]{:S(2)}) copy-start(f32[4096]{0:T(1024)} %copy-done.4) | copy-start | bytes 49156
  408.2 21.6 %copy-start.9 = (f32[4096]{0:T(1024)S(1)}, f32[4096]{0:T(1024)}, u32[]{:S(2)}) copy-start(f32[4096]{0:T(1024)} %copy-done.8) | copy-start | bytes 49156
  408.2 21.6 %copy-start.10 = (f32[4096]{0:T(1024)S(1)}, f32[4096]{0:T(1024)}, u32[]{:S(2)}) copy-start(f32[4096]{0:T(1024)} %get-tuple-element.80) | copy-start | bytes 49156
  408.2 21.6 %copy-start.11 = (f32[4096]{0:T(1024)S(1)}, f32[4096]{0:T(1024)}, u32[]{:S(2)}) copy-start(f32[4096]{0:T(1024)} %get-tuple-element.85) | copy-start | bytes 49156
  408.2 21.6 %copy-start.21 = (f32[32]{0:T(128)S(1)}, f32[32]{0:T(128)}, u32[]{:S(2)}) copy-start(f32[32]{0:T(128)} %copy-done.20) | copy-start | bytes 388
  426.8 7.4 %copy-start.23 = (s32[32]{0:T(128)S(1)}, s32[32]{0:T(128)}, u32[]{:S(2)}) copy-start(s32[32]{0:T(128)} %copy-done.22) | copy-start | bytes 388
  426.8 7.4 %copy-start.25 = (s32[80]{0:T(128)S(1)}, s32[80]{0:T(128)}, u32[]{:S(2)}) copy-start(s32[80]{0:T(128)} %copy-done.24) | copy-start | bytes 964
  426.8 8.1 %copy-start.16 = (f32[32,1]{1,0:T(8,128)S(1)}, f32[32,1]{1,0:T(8,128)}, u32[]{:S(2)}) copy-start(f32[32,1]{1,0:T(8,128)} %copy.39) | copy-start | bytes 388
  426.9 8.2 %copy-start.18 = (pred[32,80]{1,0:T(8,128)(4,1)S(1)}, pred[32,80]{1,0:T(8,128)(4,1)}, u32[]{:S(2)}) copy-start(pred[32,80]{1,0:T(8,128)(4,1)} %copy-done.17) | copy-start | bytes 7684
  460.7 33.8 %copy-start.15 = (s32[2,2,8,128]{3,2,1,0:T(8,128)S(1)}, s32[2,2,8,128]{3,2,1,0:T(8,128)}, u32[]{:S(2)}) copy-start(s32[2,2,8,128]{3,2,1,0:T(8,128)} %get-tuple-element.90) | copy-start | bytes 49156
  460.7 33.9 %copy-start.7 = (s32[4096]{0:T(1024)S(1)}, s32[4096]{0:T(1024)}, u32[]{:S(2)}) copy-start(s32[4096]{0:T(1024)} %param.8) | copy-start | bytes 49156
  460.7 33.9 %copy-start.14 = (s32[2,2,8,128]{3,1,2,0:T(2,128)S(1)}, s32[2,2,8,128]{3,1,2,0:T(2,128)}, u32[]{:S(2)}) copy-start(s32[2,2,8,128]{3,1,2,0:T(2,128)} %copy-done.13) | copy-start | bytes 49156
  489.5 11.9 %all-to-all-start.6 = ((f32[32,1,930]{2,1,0:T(1,128)}), f32[32,1,930]{2,1,0:T(1,128)S(1)}, u32[]{:S(2)}, u32[]{:S(2)}) async-start(f32[32,1,930]{2,1,0:T(1,128)} %copy.40), calls=%async_computation.6 | async-start | bytes 262144 | tf_op jit(solution)/shard_map/all_to_all | solution.py:57
  503.2 95.5 %all-to-all-start.7 = ((bf16[32,80,768]{2,1,0:T(8,128)(2,1)}), bf16[32,80,768]{2,1,0:T(8,128)(2,1)}, u32[]{:S(2)}, u32[]{:S(2)}) async-start(bf16[32,80,768]{2,1,0:T(8,128)(2,1)} %bitcast.99), calls=%async_computation.7 | async-start | bytes 7864320 | tf_op jit(solution)/shard_map/all_to_all | solution.py:57
  508.3 18.2 %copy-start.12 = (f32[4096]{0:T(1024)S(1)}, f32[4096]{0:T(1024)}, u32[]{:S(2)}) copy-start(f32[4096]{0:T(1024)} %get-tuple-element.79) | copy-start | bytes 49156
  599.4 29.1 %all-to-all-start.8 = ((f32[32,1,770]{2,1,0:T(1,128)}), f32[32,1,770]{2,1,0:T(1,128)S(1)}, u32[]{:S(2)}, u32[]{:S(2)}) async-start(f32[32,1,770]{2,1,0:T(1,128)} %broadcast_in_dim.67), calls=%async_computation.8 | async-start | bytes 229376 | tf_op jit(solution)/shard_map/all_to_all | solution.py:57
  605.7 24.5 %copy-start.27 = (s32[32]{0:T(128)S(1)}, s32[32]{0:T(128)}, u32[]{:S(2)}) copy-start(s32[32]{0:T(128)} %copy-done.26) | copy-start | bytes 388

commit v2 on v1

--- a/solution.py
+++ b/solution.py
@@ -1,6 +1,10 @@
+import functools
+
 import jax
 import jax.numpy as jnp
 from jax import lax
+from jax.experimental import pallas as pl
+from jax.experimental.pallas import tpu as pltpu
 from jax.sharding import PartitionSpec as P
 
 AUX_WEIGHT = 0.01
@@ -32,8 +36,103 @@
     return hot, pos_hot, counts, position, slot_tok
 
 
-def rows_of(source, index):
-    return source.at[index].get(mode='promise_in_bounds')
+GROUP = 4
+DEPTH = 1024
+
+
+def first_exchange(n_dev, width, slot_ref, x_ref, dy_ref, x_got, dy_got, x_late, dy_late, stage, total,
+                   send_sem, recv_sem, own_sem, late_sem):
+    me = lax.axis_index('ep')
+    tokens = x_ref.shape[0]
+    rows = GROUP * width
+    n_groups = n_dev // GROUP
+    got = (x_got, dy_got)
+    late = (x_late, dy_late)
+    block = lambda first, count: pl.ds(pl.multiple_of(first * width, 8), count * width)
+
+    def group_of(i):
+        return lax.rem(me // GROUP + n_groups // 2 + i, n_groups)
+
+    def fill(k, i):
+        group = group_of(i)
+        index = slot_ref[k // 2, block(group * GROUP, GROUP), :]
+        source = (x_ref, dy_ref)[k % 2]
+        total[...] = jnp.zeros_like(total)
+
+        def add(j, carry):
+            first = j * DEPTH
+            token = lax.broadcasted_iota(jnp.int32, (rows, DEPTH), 1) + first
+            pick = jnp.where(token == index, 1.0, 0.0).astype(BF)
+            total[...] += jnp.dot(pick, source[pl.ds(pl.multiple_of(first, DEPTH), DEPTH), :], preferred_element_type=F32)
+            return carry
+
+        lax.fori_loop(0, tokens // DEPTH, add, 0)
+        stage[k, block(group * GROUP, GROUP), :] = total[...].astype(BF)
+
+    def send(k, i):
+        group = group_of(i)
+        if k >= 2:
+            where = block(group * GROUP, GROUP)
+            pltpu.make_async_copy(stage.at[k, where], late[k - 2].at[where], late_sem.at[k - 2]).start()
+            return
+        for j in range(GROUP):
+            peer = group * GROUP + j
+            source = stage.at[k, block(peer, 1)]
+            target = got[k].at[block(me, 1)]
+
+            @pl.when(peer != me)
+            def _():
+                pltpu.make_async_remote_copy(source, target, send_sem.at[k], recv_sem.at[k], device_id=(peer,),
+                                             device_id_type=pl.DeviceIdType.MESH).start()
+
+            @pl.when(peer == me)
+            def _():
+                pltpu.make_async_copy(source, target, own_sem.at[k]).start()
+
+    for k in range(4):
+        fill(k, 0)
+        if k > 0:
+            send(k - 1, n_groups - 1)
+
+        def step(i, carry, k=k):
+            fill(k, i)
+            send(k, i - 1)
+            return carry
+
+        lax.fori_loop(1, n_groups, step, 0)
+    send(3, n_groups - 1)
+    for k in range(2):
+        others = got[k].at[block(0, n_dev - 1)]
+        pltpu.make_async_copy(stage.at[k + 2], late[k], late_sem.at[k]).wait()
+        pltpu.make_async_copy(stage.at[k, block(0, 1)], got[k].at[block(0, 1)], own_sem.at[k]).wait()
+        pltpu.make_async_copy(others, others, send_sem.at[k]).wait()
+        pltpu.make_async_copy(others, others, recv_sem.at[k]).wait()
+
+
+def start_rows(n_dev, slot_tok, x_tokens, grad_y):
+    width = slot_tok.shape[1] // CHUNKS
+    tokens, d_model = x_tokens.shape
+    n_rows = n_dev * width
+    slots = slot_tok.reshape(n_dev, CHUNKS, width).transpose(1, 0, 2).reshape(CHUNKS, n_rows, 1)
+    vmem = pl.BlockSpec(memory_space=pltpu.VMEM)
+    hbm = pl.BlockSpec(memory_space=pl.ANY)
+    out = jax.ShapeDtypeStruct((n_rows, d_model), BF)
+    return pl.pallas_call(
+        functools.partial(first_exchange, n_dev, width),
+        out_shape=[out] * 4,
+        in_specs=[vmem] * 3,
+        out_specs=[hbm] * 4,
+        scratch_shapes=[
+            pltpu.VMEM((4, n_rows, d_model), BF),
+            pltpu.VMEM((GROUP * width, d_model), F32),
+            pltpu.SemaphoreType.DMA((2,)),
+            pltpu.SemaphoreType.DMA((2,)),
+            pltpu.SemaphoreType.DMA((2,)),
+            pltpu.SemaphoreType.DMA((2,)),
+        ],
+        compiler_params=pltpu.CompilerParams(has_side_effects=True, vmem_limit_bytes=60 * 2 ** 20),
+        cost_estimate=pl.CostEstimate(flops=8 * n_rows * tokens * d_model, bytes_accessed=40 * 2 ** 20, transcendentals=0),
+    )(slots, x_tokens, grad_y)
 
 
 def router(rows, w_router):
@@ -61,22 +160,13 @@
         all_counts = exchange(jnp.broadcast_to(counts[None, :], (n_dev, num_experts)))
 
         n_rows = n_dev * width
-        first = slot_tok[:, :width]
-        second = slot_tok[:, width:]
-
-        def picked(source, index):
-            return rows_of(source, index.reshape(-1)).reshape(n_dev, index.shape[1], d_model)
-
-        x_first, all_counts = lax.optimization_barrier((picked(x_tokens, first), all_counts))
-        x_first = exchange(x_first).reshape(n_rows, d_model)
+        slot_tok, all_counts = lax.optimization_barrier((slot_tok, all_counts))
+        x_first, dy_first, x_send, dy_send = start_rows(n_dev, slot_tok, x_tokens, grad_y)
         arriving = lax.dynamic_index_in_dim(all_counts, me, 1, keepdims=False)
         load_frac = jnp.sum(all_counts, axis=0).astype(F32) / total_tok
-        dy_first, x_first = lax.optimization_barrier((picked(grad_y, first), x_first))
-        dy_first = exchange(dy_first).reshape(n_rows, d_model)
-        x_last, dy_first = lax.optimization_barrier((picked(x_tokens, second), dy_first))
-        x_last = exchange(x_last).reshape(n_rows, d_model)
-        dy_last, x_last = lax.optimization_barrier((picked(grad_y, second), x_last))
-        dy_last = exchange(dy_last).reshape(n_rows, d_model)
+        x_last = exchange(x_send.reshape(n_dev, width, d_model)).reshape(n_rows, d_model)
+        dy_send, x_last = lax.optimization_barrier((dy_send, x_last))
+        dy_last = exchange(dy_send.reshape(n_dev, width, d_model)).reshape(n_rows, d_model)
 
         prob, log_norm = router(x_tokens, w_router)
         gate = jnp.sum(prob * hot_f, axis=-1)

time: 643 us -> 655 us (1.019)
  Pallas kernels: 0 us -> 208 us
  waiting for transfers between devices: 189 us -> 76 us
  local copies, waits for them, and re-layouts: 77.2 us -> 9.71 us
  starting transfers between devices: 49.9 us -> 39.2 us
  matrix products: 304 us -> 296 us
    pallas_call x0 -> x1, Pallas kernels: none -> 208 us  [start_rows(): pl.pallas_call(functools.partial(first_exchange, n_dev, width), out_shape...]
    all_to_all x9 -> x7, waiting for transfers between devices: 189 us -> 76 us  [exchange(): return lax.all_to_all(rows, 'ep', 0, 0, tiled=True)]
    gather x4 -> x0, local copies, waits for them, and re-layouts: 55.6 us -> none  [rows_of(): return source.at[index].get(mode='promise_in_bounds')]
    all_to_all x9 -> x7, starting transfers between devices: 49.9 us -> 39.2 us  [exchange(): return lax.all_to_all(rows, 'ep', 0, 0, tiled=True)]
    convert_element_type x1 -> x0, local copies, waits for them, and re-layouts: 6.7 us -> none  [forward(): dy_f = dy.astype(F32)]
  transfers between devices with their start and end apart: 9 -> 7, of which waited for: 6 -> 5; matrix products, arithmetic and copies ran while one was open for 60% -> 48% of each run, Pallas kernels for 0% -> 0%
where the time goes in v2:
time: 655 us; the launch traced here: 647 us
  matrix products  296 us (45%)
  Pallas kernels  208 us (32%)
  waiting for transfers between devices  76 us (12%)
  starting transfers between devices  39.2 us (6%)
  other arithmetic  12.6 us (2%)
  local copies, waits for them, and re-layouts  9.71 us (1%)
    pallas_call x1, Pallas kernels, start_rows(): pl.pallas_call(functools.partial(first_exchange, n_dev, width), out_shape...  208 us
    all_to_all x7, waiting for transfers between devices, exchange(): return lax.all_to_all(rows, 'ep', 0, 0, tiled=True)  76 us
    dot_general x2, matrix products, placed(): jnp.dot(pick, back.reshape(n_rows, d_model), preferred_element_type=F32)  46 us
    dot_general x2, matrix products, backward(): jnp.einsum('nd,fd->nf', scaled, w_out, preferred_element_type=F32)  42.3 us
    all_to_all x7, starting transfers between devices, exchange(): return lax.all_to_all(rows, 'ep', 0, 0, tiled=True)  39.2 us
    dot_general x2, matrix products, forward(): jnp.dot(rows, w_in, preferred_element_type=F32)  37.6 us
    dot_general x2, matrix products, forward(): expert_out = jnp.dot(hidden, w_out, preferred_element_type=F32).astype(BF)  33.9 us
    dot_general x2, matrix products, backward(): jnp.einsum('nf,df->nd', d_pre, w_in, preferred_element_type=F32).astype(BF)  33.5 us
  transfers between devices with their start and end apart: 7, of which 5 were waited for; matrix products, arithmetic and copies ran while one was open for 48% of the time, Pallas kernels for 0%

profile of v2, /device:TPU:3, one launch (start us, length us, event | category | flops | bytes accessed | tf_op | source)
XLA Modules:
  0.0 647.1 jit_solution(10202446455430266486)
XLA Ops:
  0.7 0.8 eq.77
  1.4 0.3 convolution_bitcast_fusion
  1.7 0.3 slice_reduce_fusion
  2.0 0.2 slice_reduce_fusion.2
  2.2 0.1 multiply_reduce_fusion.4
  2.3 0.6 broadcast_in_dim.51
  2.9 6.4 all-to-all-start
  9.3 0.2 multiply_reduce_fusion.1
  9.6 4.7 fusion.94
  14.4 0.6 fusion.22
  15.2 2.8 reshape.263.slot_ref
  18.0 208.5 %shard_map.109 = (bf16[2560,768]{1,0:T(8,128)(2,1)}, bf16[2560,768]{1,0:T(8,128)(2,1)}, bf16[2560,768]{1,0:T(8,128)(2,1)}, bf16[2560,768]{1,0:T(8,128)(2,1)}) custom-call(s32[2,2560,1]{2,1,0:T(8,128)} %reshape.263.slot_ref, bf16[4096,768]{1,0:T(8,128)(2,1)} %x_ref.1, bf16[4096,768]{1,0:T(8,128)(2,1)} %dy_ref.1), custom_call_target="tpu_custom_call" | custom-call | flops 64424509440 | bytes 41943040 | tf_op jit(solution)/shard_map/pallas_call | solution.py:120
  226.5 6.6 %all-to-all-start.1 = ((bf16[32,80,768]{2,1,0:T(8,128)(2,1)}), bf16[32,80,768]{2,1,0:T(8,128)(2,1)}, u32[]{:S(2)}, u32[]{:S(2)}) async-start(bf16[32,80,768]{2,1,0:T(8,128)(2,1)} %bitcast.103), calls=%async_computation.1 | async-start | bytes 7864320 | tf_op jit(solution)/shard_map/all_to_all | solution.py:156
  233.2 0.1 fusion.43
  233.3 0.6 add_select_fusion.1
  234.0 18.9 %maximum_convert_fusion.1 = bf16[2560,3072]{1,0:T(8,128)(2,1)} fusion(bf16[2560,768]{1,0:T(8,128)(2,1)} %get-tuple-element.32, bf16[1,768,3072]{2,1,0:T(8,128)(2,1)} %param.9), kind=kOutput, calls=%fused_computation.7 | convolution fusion | flops 12095324160 | bytes 24379392 | tf_op jit(solution)/shard_map/dot_general | solution.py:183
  252.9 16.0 %fusion.4 = f32[2560]{0:T(1024)S(1)} fusion(bf16[2560,768]{1,0:T(8,128)(2,1)S(1)} %copy-done.12, bf16[2560,3072]{1,0:T(8,128)(2,1)} %maximum_convert_fusion.1, bf16[1,3072,768]{2,1,0:T(8,128)(2,1)S(1)} %bitcast.121), kind=kOutput, calls=%fused_computation.15 | convolution fusion | flops 12089423872 | bytes 24389632 | tf_op jit(solution)/shard_map/dot_general | solution.py:184
  269.0 0.2 dynamic-slice_reduce_fusion
  269.4 1.0 fusion.91
  270.5 3.4 fusion.96
  273.9 0.6 multiply_reduce_fusion.5
  274.6 45.7 %all-to-all-done.1 = bf16[32,80,768]{2,1,0:T(8,128)(2,1)} async-done(((bf16[32,80,768]{2,1,0:T(8,128)(2,1)}), bf16[32,80,768]{2,1,0:T(8,128)(2,1)}, u32[]{:S(2)}, u32[]{:S(2)}) %all-to-all-start.1) | async-done | bytes 3932192 | tf_op jit(solution)/shard_map/all_to_all | solution.py:156
  320.2 5.6 all-to-all-start.2
  325.9 3.4 fusion.95
  329.3 0.2 multiply_reduce_fusion.2
  329.5 20.7 %select_convert_fusion.1 = bf16[2560,3072]{1,0:T(8,128)(2,1)} fusion(bf16[2560,3072]{1,0:T(8,128)(2,1)} %maximum_convert_fusion.1, bf16[1,3072,768]{2,1,0:T(8,128)(2,1)} %param.10, bf16[2560,768]{1,0:T(8,128)(2,1)} %get-tuple-element.33, f32[2560]{0:T(1024)S(1)} %get-tuple-element.83, pred[2560]{0:T(1024)(128)(4,1)S(1)} %lt.95), kind=kOutput, calls=%fused_computation.5 | convolution fusion | flops 12111052800 | bytes 40120832 | tf_op jit(solution)/shard_map/nd,fd->nf/dot_general | solution.py:195
  350.2 17.6 %fusion.97 = f32[768,3072]{1,0:T(8,128)} fusion(bf16[2560,768]{1,0:T(8,128)(2,1)S(1)} %copy-done.1, bf16[2560,3072]{1,0:T(8,128)(2,1)} %select_convert_fusion.1), kind=kOutput, calls=%fused_computation.156 | convolution fusion | flops 12079595520 | bytes 29097984 | tf_op jit(solution)/shard_map/nd,nf->df/dot_general | solution.py:206
  367.9 15.7 %convolution_convert_fusion.1 = bf16[2560,768]{1,0:T(8,128)(2,1)} fusion(bf16[2560,3072]{1,0:T(8,128)(2,1)S(1)} %copy-done.11, bf16[1,768,3072]{2,1,0:T(8,128)(2,1)} %param.9), kind=kOutput, calls=%fused_computation.28 | convolution fusion | flops 12081561600 | bytes 24379392 | tf_op jit(solution)/shard_map/nf,df->nd/dot_general | solution.py:197
  383.6 2.9 fusion.47
  386.5 18.7 %maximum_convert_fusion = bf16[2560,3072]{1,0:T(8,128)(2,1)} fusion(bf16[2560,768]{1,0:T(8,128)(2,1)} %bitcast.8, bf16[1,768,3072]{2,1,0:T(8,128)(2,1)} %param.9), kind=kOutput, calls=%fused_computation.6 | convolution fusion | flops 12095324160 | bytes 24379392 | tf_op jit(solution)/shard_map/dot_general | solution.py:183
  405.3 7.7 %all-to-all-done.2 = bf16[32,80,768]{2,1,0:T(8,128)(2,1)} async-done(((bf16[32,80,768]{2,1,0:T(8,128)(2,1)}), bf16[32,80,768]{2,1,0:T(8,128)(2,1)}, u32[]{:S(2)}, u32[]{:S(2)}) %all-to-all-start.2) | async-done | bytes 3932192 | tf_op jit(solution)/shard_map/all_to_all | solution.py:156
  412.9 5.1 all-to-all-start.3
  418.0 17.9 %fusion.9 = f32[2560]{0:T(1024)S(1)} fusion(bf16[32,80,768]{2,1,0:T(8,128)(2,1)} %all-to-all-done.2, bf16[2560,3072]{1,0:T(8,128)(2,1)} %maximum_convert_fusion, bf16[1,3072,768]{2,1,0:T(8,128)(2,1)} %param.10), kind=kOutput, calls=%fused_computation.23 | convolution fusion | flops 12089423872 | bytes 24389632 | tf_op jit(solution)/shard_map/dot_general | solution.py:184
  436.0 2.9 convolution_add_fusion
  439.0 4.0 fusion.29
  443.0 0.2 copy.44
  443.1 0.1 reshape.255
  443.4 0.6 broadcast_in_dim.58
  444.0 0.1 concatenate.7
  444.2 4.0 fusion.8
  448.2 21.6 %select_convert_fusion = bf16[2560,3072]{1,0:T(8,128)(2,1)} fusion(bf16[2560,3072]{1,0:T(8,128)(2,1)} %maximum_convert_fusion, bf16[2560,768]{1,0:T(8,128)(2,1)} %bitcast.101, bf16[1,3072,768]{2,1,0:T(8,128)(2,1)} %param.10), kind=kOutput, calls=%fused_computation.4 | convolution fusion | flops 12103188480 | bytes 40108032 | tf_op jit(solution)/shard_map/nd,fd->nf/dot_general | solution.py:195
  469.7 17.9 %convolution_convert_fusion = bf16[2560,768]{1,0:T(8,128)(2,1)} fusion(bf16[2560,3072]{1,0:T(8,128)(2,1)} %select_convert_fusion, bf16[1,768,3072]{2,1,0:T(8,128)(2,1)} %param.9), kind=kOutput, calls=%fused_computation.27 | convolution fusion | flops 12081561600 | bytes 24379392 | tf_op jit(solution)/shard_map/nf,df->nd/dot_general | solution.py:197
  487.6 17.6 %all-to-all-done.3 = bf16[32,80,768]{2,1,0:T(8,128)(2,1)} async-done(((bf16[32,80,768]{2,1,0:T(8,128)(2,1)}), bf16[32,80,768]{2,1,0:T(8,128)(2,1)}, u32[]{:S(2)}, u32[]{:S(2)}) %all-to-all-start.3) | async-done | bytes 3932192 | tf_op jit(solution)/shard_map/all_to_all | solution.py:156
  505.2 0.8 copy.46
  506.0 5.0 all-to-all-start.4
  511.1 4.5 fusion.11
  515.6 2.4 all-to-all-done.4
  518.0 0.1 slice_reduce_fusion.1
  518.1 1.6 fusion.27
  519.8 5.4 all-to-all-start.5
  525.3 20.0 %fusion.88 = f32[3072,768]{1,0:T(8,128)} fusion(bf16[2560,3072]{1,0:T(8,128)(2,1)} %maximum_convert_fusion.1, bf16[2560,768]{1,0:T(8,128)(2,1)} %get-tuple-element.33, f32[2560]{0:T(1024)S(1)} %get-tuple-element.83, pred[2560]{0:T(1024)(128)(4,1)S(1)} %lt.95), kind=kOutput, calls=%fused_computation.151 | convolution fusion | flops 12087459840 | bytes 29110784 | tf_op jit(solution)/shard_map/nf,nd->fd/dot_general | solution.py:229
  545.3 18.4 %add_bitcast_fusion.1 = f32[1,768,3072]{2,1,0:T(8,128)} fusion(f32[768,3072]{1,0:T(8,128)S(1)} %bitcast.123, bf16[2560,768]{1,0:T(8,128)(2,1)} %bitcast.8, bf16[2560,3072]{1,0:T(8,128)(2,1)} %select_convert_fusion), kind=kOutput, calls=%fused_computation.14 | convolution fusion | flops 12081954816 | bytes 38535168 | tf_op jit(solution)/shard_map/nd,nf->df/dot_general | solution.py:201
  563.7 1.9 fusion.33
  565.7 20.8 %add_bitcast_fusion = f32[1,3072,768]{2,1,0:T(8,128)} fusion(f32[3072,768]{1,0:T(8,128)} %fusion.88, bf16[2560,3072]{1,0:T(8,128)(2,1)} %maximum_convert_fusion, bf16[2560,768]{1,0:T(8,128)(2,1)} %fusion.11), kind=kOutput, calls=%fused_computation.13 | convolution fusion | flops 12081954816 | bytes 38535168 | tf_op jit(solution)/shard_map/nf,nd->fd/dot_general | solution.py:202
  586.5 23.3 %fusion.12 = f32[4096,768]{1,0:T(8,128)} fusion(f32[4096,768]{1,0:T(8,128)S(1)} %fusion.33, bf16[2560,768]{1,0:T(8,128)(2,1)} %bitcast.17, s32[4096]{0:T(1024)S(1)} %copy-done.8), kind=kOutput, calls=%fused_computation.26 | convolution fusion | flops 16119758848 | bytes 29114368 | tf_op jit(solution)/shard_map/dot_general | solution.py:238
  609.8 2.7 all-to-all-done.5
  612.4 0.7 broadcast_in_dim.115
  613.1 5.0 all-to-all-start.6
  618.1 22.8 %add_convert_fusion = bf16[4096,768]{1,0:T(8,128)(2,1)} fusion(f32[4096,768]{1,0:T(8,128)} %fusion.12, bf16[2560,768]{1,0:T(8,128)(2,1)} %bitcast.18, s32[4096]{0:T(1024)S(1)} %copy-done.7), kind=kOutput, calls=%fused_computation.10 | convolution fusion | flops 16122904576 | bytes 22822912 | tf_op jit(solution)/shard_map/dot_general | solution.py:238
  640.9 0.1 fusion.83
  641.0 0.7 slice.49
  641.7 0.1 reshape.260
  641.9 0.8 copy.47
  642.6 0.6 multiply_reduce_fusion.6
  (71 shorter events, 1.2 us)
Async XLA Ops:
  0.6 9.0 %copy-start = (f32[768,32]{0,1:T(8,128)S(1)}, f32[768,32]{0,1:T(8,128)}, u32[]{:S(2)}) copy-start(f32[768,32]{0,1:T(8,128)} %param.7) | copy-start | bytes 294916
  0.6 13.7 %copy-start.2 = (s32[4096]{0:T(1024)S(1)}, s32[4096]{0:T(1024)}, u32[]{:S(2)}) copy-start(s32[4096]{0:T(1024)} %param.8) | copy-start | bytes 49156
  2.9 12.2 %all-to-all-start = ((s32[32,1,32]{2,1,0:T(1,128)}), s32[32,1,32]{2,1,0:T(1,128)S(1)}, u32[]{:S(2)}, u32[]{:S(2)}) async-start(s32[32,1,32]{2,1,0:T(1,128)} %broadcast_in_dim.51), calls=%async_computation | async-start | bytes 32768 | tf_op jit(solution)/shard_map/all_to_all | solution.py:156
  9.6 223.7 %copy-start.5 = (s32[2,2,8,128]{3,1,2,0:T(2,128)}, s32[2,2,8,128]{3,1,2,0:T(2,128)S(1)}, u32[]{:S(2)}) copy-start(s32[2,2,8,128]{3,1,2,0:T(2,128)S(1)} %copy.52) | copy-start | bytes 49156
  226.5 26.4 %slice-start = ((s8[4718592]{0:T(1024)(128)(4,1)}), s8[524288]{0:T(1024)(128)(4,1)S(1)}, s32[]{:S(2)}) async-start(s8[4718592]{0:T(1024)(128)(4,1)} %bitcast.120), calls=%async_computation.7 | async-start | bytes 1048576
  226.5 93.7 %all-to-all-start.1 = ((bf16[32,80,768]{2,1,0:T(8,128)(2,1)}), bf16[32,80,768]{2,1,0:T(8,128)(2,1)}, u32[]{:S(2)}, u32[]{:S(2)}) async-start(bf16[32,80,768]{2,1,0:T(8,128)(2,1)} %bitcast.103), calls=%async_computation.1 | async-start | bytes 7864320 | tf_op jit(solution)/shard_map/all_to_all | solution.py:156
  233.9 35.5 %copy-start.9 = (s32[32]{0:T(128)}, s32[32]{0:T(128)S(1)}, u32[]{:S(2)}) copy-start(s32[32]{0:T(128)S(1)} %reduce_sum.169) | copy-start | bytes 388
  234.0 18.9 %slice-start.1 = ((s8[4718592]{0:T(1024)(128)(4,1)}), s8[4194304]{0:T(1024)(128)(4,1)S(1)}, s32[]{:S(2)}) async-start(s8[4718592]{0:T(1024)(128)(4,1)} %bitcast.120), calls=%async_computation.8 | async-start | bytes 8388608
  234.0 18.9 %copy-start.12 = (bf16[2560,768]{1,0:T(8,128)(2,1)S(1)}, bf16[2560,768]{1,0:T(8,128)(2,1)}, u32[]{:S(2)}) copy-start(bf16[2560,768]{1,0:T(8,128)(2,1)} %get-tuple-element.33) | copy-start | bytes 11796484
  320.2 92.7 %all-to-all-start.2 = ((bf16[32,80,768]{2,1,0:T(8,128)(2,1)}), bf16[32,80,768]{2,1,0:T(8,128)(2,1)}, u32[]{:S(2)}, u32[]{:S(2)}) async-start(bf16[32,80,768]{2,1,0:T(8,128)(2,1)} %bitcast.102), calls=%async_computation.2 | async-start | bytes 7864320 | tf_op jit(solution)/shard_map/all_to_all | solution.py:156
  329.5 20.7 %copy-start.1 = (bf16[2560,768]{1,0:T(8,128)(2,1)S(1)}, bf16[2560,768]{1,0:T(8,128)(2,1)}, u32[]{:S(2)}) copy-start(bf16[2560,768]{1,0:T(8,128)(2,1)} %get-tuple-element.32) | copy-start | bytes 11796484
  350.2 17.6 %copy-start.11 = (bf16[2560,3072]{1,0:T(8,128)(2,1)S(1)}, bf16[2560,3072]{1,0:T(8,128)(2,1)}, u32[]{:S(2)}) copy-start(bf16[2560,3072]{1,0:T(8,128)(2,1)} %select_convert_fusion.1) | copy-start | bytes 47185924
  412.9 92.3 %all-to-all-start.3 = ((bf16[32,80,768]{2,1,0:T(8,128)(2,1)}), bf16[32,80,768]{2,1,0:T(8,128)(2,1)}, u32[]{:S(2)}, u32[]{:S(2)}) async-start(bf16[32,80,768]{2,1,0:T(8,128)(2,1)} %bitcast.104), calls=%async_computation.3 | async-start | bytes 7864320 | tf_op jit(solution)/shard_map/all_to_all | solution.py:156
  487.6 30.5 %copy-start.3 = (s32[4096]{0:T(1024)S(1)}, s32[4096]{0:T(1024)}, u32[]{:S(2)}) copy-start(s32[4096]{0:T(1024)} %param.8) | copy-start | bytes 49156
  487.6 30.5 %copy-start.6 = (s32[2,2,8,128]{3,1,2,0:T(2,128)S(1)}, s32[2,2,8,128]{3,1,2,0:T(2,128)}, u32[]{:S(2)}) copy-start(s32[2,2,8,128]{3,1,2,0:T(2,128)} %copy-done.5) | copy-start | bytes 49156
  506.0 11.9 %all-to-all-start.4 = ((f32[32,1,930]{2,1,0:T(1,128)}), f32[32,1,930]{2,1,0:T(1,128)S(1)}, u32[]{:S(2)}, u32[]{:S(2)}) async-start(f32[32,1,930]{2,1,0:T(1,128)} %copy.46), calls=%async_computation.4 | async-start | bytes 262144 | tf_op jit(solution)/shard_map/all_to_all | solution.py:156
  519.8 25.5 %slice-start.2 = ((s8[9437184]{0:T(1024)(128)(4,1)}), s8[1048576]{0:T(1024)(128)(4,1)S(1)}, s32[]{:S(2)}) async-start(s8[9437184]{0:T(1024)(128)(4,1)} %bitcast.122), calls=%async_computation.9 | async-start | bytes 2097152
  519.8 92.7 %all-to-all-start.5 = ((bf16[32,80,768]{2,1,0:T(8,128)(2,1)}), bf16[32,80,768]{2,1,0:T(8,128)(2,1)}, u32[]{:S(2)}, u32[]{:S(2)}) async-start(bf16[32,80,768]{2,1,0:T(8,128)(2,1)} %bitcast.105), calls=%async_computation.5 | async-start | bytes 7864320 | tf_op jit(solution)/shard_map/all_to_all | solution.py:156
  525.2 20.0 %copy-start.4 = (f32[4096]{0:T(1024)S(1)}, f32[4096]{0:T(1024)}, u32[]{:S(2)}) copy-start(f32[4096]{0:T(1024)} %get-tuple-element.79) | copy-start | bytes 49156
  525.2 20.0 %slice-start.3 = ((s8[9437184]{0:T(1024)(128)(4,1)}), s8[4194304]{0:T(1024)(128)(4,1)S(1)}, s32[]{:S(2)}) async-start(s8[9437184]{0:T(1024)(128)(4,1)} %bitcast.122), calls=%async_computation.10 | async-start | bytes 8388608
  525.3 20.0 %slice-start.4 = ((s8[9437184]{0:T(1024)(128)(4,1)}), s8[4194304]{0:T(1024)(128)(4,1)S(1)}, s32[]{:S(2)}) async-start(s8[9437184]{0:T(1024)(128)(4,1)} %bitcast.122), calls=%async_computation.11 | async-start | bytes 8388608
  565.7 20.8 %copy-start.8 = (s32[4096]{0:T(1024)S(1)}, s32[4096]{0:T(1024)}, u32[]{:S(2)}) copy-start(s32[4096]{0:T(1024)} %get-tuple-element.87) | copy-start | bytes 49156
  586.5 31.6 %copy-start.7 = (s32[4096]{0:T(1024)S(1)}, s32[4096]{0:T(1024)}, u32[]{:S(2)}) copy-start(s32[4096]{0:T(1024)} %get-tuple-element.86) | copy-start | bytes 49156
  613.1 27.8 %all-to-all-start.6 = ((f32[32,1,770]{2,1,0:T(1,128)}), f32[32,1,770]{2,1,0:T(1,128)S(1)}, u32[]{:S(2)}, u32[]{:S(2)}) async-start(f32[32,1,770]{2,1,0:T(1,128)} %broadcast_in_dim.115), calls=%async_computation.6 | async-start | bytes 229376 | tf_op jit(solution)/shard_map/all_to_all | solution.py:156
  618.1 24.5 %copy-start.10 = (s32[32]{0:T(128)S(1)}, s32[32]{0:T(128)}, u32[]{:S(2)}) copy-start(s32[32]{0:T(128)} %copy-done.9) | copy-start | bytes 388

commit v3 on v2

--- a/solution.py
+++ b/solution.py
@@ -36,18 +36,33 @@
     return hot, pos_hot, counts, position, slot_tok
 
 
-GROUP = 4
+def rows_of(source, index):
+    return source.at[index].get(mode='promise_in_bounds')
+
+
+GROUP = 8
 DEPTH = 1024
 
 
-def first_exchange(n_dev, width, slot_ref, x_ref, dy_ref, x_got, dy_got, x_late, dy_late, stage, total,
-                   send_sem, recv_sem, own_sem, late_sem):
+def first_exchange(n_dev, width, count_ref, slot_ref, x_ref, dy_hbm, count_got, x_got, dy_got, x_late, dy_ref, stage, total,
+                   send_sem, recv_sem, own_sem, late_sem, load_sem):
     me = lax.axis_index('ep')
+    load = pltpu.make_async_copy(dy_hbm, dy_ref, load_sem)
+    load.start()
     tokens = x_ref.shape[0]
     rows = GROUP * width
     n_groups = n_dev // GROUP
     got = (x_got, dy_got)
-    late = (x_late, dy_late)
+    tile = count_ref.shape[0]
+
+    def tell(k, carry):
+        peer = lax.rem(me + k, n_dev)
+        pltpu.make_async_remote_copy(count_ref, count_got.at[pl.ds(pl.multiple_of(me * tile, tile), tile)], send_sem.at[2], recv_sem.at[2],
+                                     device_id=(peer,), device_id_type=pl.DeviceIdType.MESH).start()
+        return carry
+
+    lax.fori_loop(1, n_dev, tell, 0)
+    pltpu.make_async_copy(count_ref, count_got.at[pl.ds(pl.multiple_of(me * tile, tile), tile)], own_sem.at[2]).start()
     block = lambda first, count: pl.ds(pl.multiple_of(first * width, 8), count * width)
 
     def group_of(i):
@@ -73,7 +88,7 @@
         group = group_of(i)
         if k >= 2:
             where = block(group * GROUP, GROUP)
-            pltpu.make_async_copy(stage.at[k, where], late[k - 2].at[where], late_sem.at[k - 2]).start()
+            pltpu.make_async_copy(stage.at[k, where], x_late.at[where], late_sem).start()
             return
         for j in range(GROUP):
             peer = group * GROUP + j
@@ -89,7 +104,9 @@
             def _():
                 pltpu.make_async_copy(source, target, own_sem.at[k]).start()
 
-    for k in range(4):
+    for k in range(3):
+        if k == 1:
+            load.wait()
         fill(k, 0)
         if k > 0:
             send(k - 1, n_groups - 1)
@@ -100,16 +117,20 @@
             return carry
 
         lax.fori_loop(1, n_groups, step, 0)
-    send(3, n_groups - 1)
+    send(2, n_groups - 1)
+    pltpu.make_async_copy(stage.at[2], x_late, late_sem).wait()
+    told = count_got.at[pl.ds(0, (n_dev - 1) * tile)]
+    pltpu.make_async_copy(count_ref, count_got.at[pl.ds(0, tile)], own_sem.at[2]).wait()
+    pltpu.make_async_copy(told, told, send_sem.at[2]).wait()
+    pltpu.make_async_copy(told, told, recv_sem.at[2]).wait()
     for k in range(2):
         others = got[k].at[block(0, n_dev - 1)]
-        pltpu.make_async_copy(stage.at[k + 2], late[k], late_sem.at[k]).wait()
         pltpu.make_async_copy(stage.at[k, block(0, 1)], got[k].at[block(0, 1)], own_sem.at[k]).wait()
         pltpu.make_async_copy(others, others, send_sem.at[k]).wait()
         pltpu.make_async_copy(others, others, recv_sem.at[k]).wait()
 
 
-def start_rows(n_dev, slot_tok, x_tokens, grad_y):
+def start_rows(n_dev, counts, slot_tok, x_tokens, grad_y):
     width = slot_tok.shape[1] // CHUNKS
     tokens, d_model = x_tokens.shape
     n_rows = n_dev * width
@@ -117,22 +138,25 @@
     vmem = pl.BlockSpec(memory_space=pltpu.VMEM)
     hbm = pl.BlockSpec(memory_space=pl.ANY)
     out = jax.ShapeDtypeStruct((n_rows, d_model), BF)
+    block = jnp.pad(counts[None, :], ((0, 7), (0, 128 - counts.shape[0])))
     return pl.pallas_call(
         functools.partial(first_exchange, n_dev, width),
-        out_shape=[out] * 4,
-        in_specs=[vmem] * 3,
+        out_shape=[jax.ShapeDtypeStruct((n_dev * 8, 128), jnp.int32)] + [out] * 3,
+        in_specs=[vmem] * 3 + [hbm],
         out_specs=[hbm] * 4,
         scratch_shapes=[
-            pltpu.VMEM((4, n_rows, d_model), BF),
+            pltpu.VMEM((tokens, d_model), BF),
+            pltpu.VMEM((3, n_rows, d_model), BF),
             pltpu.VMEM((GROUP * width, d_model), F32),
-            pltpu.SemaphoreType.DMA((2,)),
-            pltpu.SemaphoreType.DMA((2,)),
-            pltpu.SemaphoreType.DMA((2,)),
-            pltpu.SemaphoreType.DMA((2,)),
+            pltpu.SemaphoreType.DMA((3,)),
+            pltpu.SemaphoreType.DMA((3,)),
+            pltpu.SemaphoreType.DMA((3,)),
+            pltpu.SemaphoreType.DMA,
+            pltpu.SemaphoreType.DMA,
         ],
         compiler_params=pltpu.CompilerParams(has_side_effects=True, vmem_limit_bytes=60 * 2 ** 20),
-        cost_estimate=pl.CostEstimate(flops=8 * n_rows * tokens * d_model, bytes_accessed=40 * 2 ** 20, transcendentals=0),
-    )(slots, x_tokens, grad_y)
+        cost_estimate=pl.CostEstimate(flops=6 * n_rows * tokens * d_model, bytes_accessed=40 * 2 ** 20, transcendentals=0),
+    )(block, slots, x_tokens, grad_y)
 
 
 def router(rows, w_router):
@@ -157,14 +181,15 @@
 
         hot, pos_hot, counts, position, slot_tok = route(expert_idx, num_experts, capacity)
         hot_f = hot.astype(F32)
-        all_counts = exchange(jnp.broadcast_to(counts[None, :], (n_dev, num_experts)))
 
         n_rows = n_dev * width
-        slot_tok, all_counts = lax.optimization_barrier((slot_tok, all_counts))
-        x_first, dy_first, x_send, dy_send = start_rows(n_dev, slot_tok, x_tokens, grad_y)
+        count_got, x_first, dy_first, x_send = start_rows(n_dev, counts, slot_tok, x_tokens, grad_y)
+        all_counts = count_got.reshape(n_dev, 8, 128)[:, 0, :num_experts]
         arriving = lax.dynamic_index_in_dim(all_counts, me, 1, keepdims=False)
         load_frac = jnp.sum(all_counts, axis=0).astype(F32) / total_tok
         x_last = exchange(x_send.reshape(n_dev, width, d_model)).reshape(n_rows, d_model)
+        late, count_got = lax.optimization_barrier((slot_tok[:, width:].reshape(-1), count_got))
+        dy_send = rows_of(grad_y, late)
         dy_send, x_last = lax.optimization_barrier((dy_send, x_last))
         dy_last = exchange(dy_send.reshape(n_dev, width, d_model)).reshape(n_rows, d_model)
 

time: 655 us -> 660 us (level)
  starting transfers between devices: 39.2 us -> 77.8 us
  Pallas kernels: 208 us -> 178 us
  waiting for transfers between devices: 76 us -> 55.8 us
  local copies, waits for them, and re-layouts: 9.71 us -> 23.7 us
    all_to_all x7 -> x6, starting transfers between devices: 39.2 us -> 77.8 us  [exchange(): return lax.all_to_all(rows, 'ep', 0, 0, tiled=True)]
    pallas_call x1, Pallas kernels: 208 us -> 178 us  [start_rows(): pl.pallas_call(functools.partial(first_exchange, n_dev, width), out_shape...]
    all_to_all x7 -> x6, waiting for transfers between devices: 76 us -> 55.8 us  [exchange(): return lax.all_to_all(rows, 'ep', 0, 0, tiled=True)]
    gather x0 -> x1, local copies, waits for them, and re-layouts: none -> 13.9 us  [rows_of(): return source.at[index].get(mode='promise_in_bounds')]
  transfers between devices with their start and end apart: 7 -> 6, of which waited for: 5 -> 5; matrix products, arithmetic and copies ran while one was open for 48% -> 49% of each run, Pallas kernels for 0% -> 0%
where the time goes in v3:
time: 660 us; the launch traced here: 651 us
  matrix products  296 us (45%)
  Pallas kernels  178 us (27%)
  starting transfers between devices  77.8 us (12%)
  waiting for transfers between devices  55.8 us (8%)
  local copies, waits for them, and re-layouts  23.7 us (4%)
  other arithmetic  14.3 us (2%)
    pallas_call x1, Pallas kernels, start_rows(): pl.pallas_call(functools.partial(first_exchange, n_dev, width), out_shape...  178 us
    all_to_all x6, starting transfers between devices, exchange(): return lax.all_to_all(rows, 'ep', 0, 0, tiled=True)  77.8 us
    all_to_all x6, waiting for transfers between devices, exchange(): return lax.all_to_all(rows, 'ep', 0, 0, tiled=True)  55.8 us
    dot_general x2, matrix products, placed(): jnp.dot(pick, back.reshape(n_rows, d_model), preferred_element_type=F32)  46 us
    dot_general x2, matrix products, backward(): jnp.einsum('nd,fd->nf', scaled, w_out, preferred_element_type=F32)  42.1 us
    dot_general x2, matrix products, forward(): jnp.dot(rows, w_in, preferred_element_type=F32)  37.6 us
    dot_general x2, matrix products, forward(): expert_out = jnp.dot(hidden, w_out, preferred_element_type=F32).astype(BF)  34.1 us
    dot_general x2, matrix products, backward(): jnp.einsum('nf,df->nd', d_pre, w_in, preferred_element_type=F32).astype(BF)  33.8 us
  transfers between devices with their start and end apart: 6, of which 5 were waited for; matrix products, arithmetic and copies ran while one was open for 49% of the time, Pallas kernels for 0%

profile of v3, /device:TPU:3, one launch (start us, length us, event | category | flops | bytes accessed | tf_op | source)
XLA Modules:
  0.0 650.9 jit_solution(17295033495090085615)
XLA Ops:
  0.7 0.8 eq.74
  1.4 0.3 convolution_bitcast_fusion
  1.7 0.3 slice_reduce_fusion
  2.0 0.2 slice_reduce_fusion.2
  2.2 0.1 multiply_reduce_fusion.4
  2.3 0.2 multiply_reduce_fusion.1
  2.5 0.8 fusion.40
  3.3 0.6 fusion.22
  4.1 2.8 reshape.277.slot_ref
  6.8 0.6 pad.4.count_ref
  7.4 177.9 %shard_map.109 = (s32[256,128]{1,0:T(8,128)}, bf16[2560,768]{1,0:T(8,128)(2,1)}, bf16[2560,768]{1,0:T(8,128)(2,1)}, bf16[2560,768]{1,0:T(8,128)(2,1)}) custom-call(s32[8,128]{1,0:T(8,128)} %pad.4.count_ref, s32[2,2560,1]{2,1,0:T(8,128)} %reshape.277.slot_ref, bf16[4096,768]{1,0:T(8,128)(2,1)} %x_ref.1, bf16[4096,768]{1,0:T(8,128)(2,1)} %dy_hbm.1), custom_call_target="tpu_custom_call" | custom-call | flops 48318382080 | bytes 41943040 | tf_op jit(solution)/shard_map/pallas_call | solution.py:142
  185.4 52.1 %all-to-all-start = ((bf16[32,80,768]{2,1,0:T(8,128)(2,1)}), bf16[32,80,768]{2,1,0:T(8,128)(2,1)}, u32[]{:S(2)}, u32[]{:S(2)}) async-start(bf16[32,80,768]{2,1,0:T(8,128)(2,1)} %bitcast.102), calls=%async_computation | async-start | bytes 7864320 | tf_op jit(solution)/shard_map/all_to_all | solution.py:180
  237.5 1.0 fusion.93
  238.6 13.9 %gather_fusion = bf16[2560,768]{1,0:T(8,128)(2,1)} fusion(bf16[4096,768]{1,0:T(8,128)(2,1)} %dy_hbm.1, s32[3072]{0:T(1024)S(1)} %pad_clamp_fusion), kind=kCustom, calls=%fused_computation | custom fusion | bytes 7874560 | tf_op jit(solution)/shard_map/gather | solution.py:40
  252.7 18.9 %maximum_convert_fusion.1 = bf16[2560,3072]{1,0:T(8,128)(2,1)} fusion(bf16[2560,768]{1,0:T(8,128)(2,1)} %get-tuple-element.30, bf16[1,768,3072]{2,1,0:T(8,128)(2,1)} %param.9), kind=kOutput, calls=%fused_computation.8 | convolution fusion | flops 12095324160 | bytes 24379392 | tf_op jit(solution)/shard_map/dot_general | solution.py:208
  271.6 16.2 %fusion.4 = f32[2560]{0:T(1024)S(1)} fusion(bf16[2560,768]{1,0:T(8,128)(2,1)S(1)} %copy-done.12, bf16[2560,3072]{1,0:T(8,128)(2,1)} %maximum_convert_fusion.1, bf16[1,3072,768]{2,1,0:T(8,128)(2,1)S(1)} %bitcast.121), kind=kOutput, calls=%fused_computation.16 | convolution fusion | flops 12089423872 | bytes 24389632 | tf_op jit(solution)/shard_map/dot_general | solution.py:209
  288.2 4.7 fusion.94
  293.0 1.0 fusion.90
  294.1 3.4 fusion.96
  297.6 0.6 multiply_reduce_fusion.5
  298.2 0.6 add_select_fusion.1
  298.8 25.7 %all-to-all-done = bf16[32,80,768]{2,1,0:T(8,128)(2,1)} async-done(((bf16[32,80,768]{2,1,0:T(8,128)(2,1)}), bf16[32,80,768]{2,1,0:T(8,128)(2,1)}, u32[]{:S(2)}, u32[]{:S(2)}) %all-to-all-start) | async-done | bytes 3932192 | tf_op jit(solution)/shard_map/all_to_all | solution.py:180
  324.5 5.5 all-to-all-start.1
  330.0 3.4 fusion.95
  333.4 0.2 multiply_reduce_fusion.2
  333.6 20.7 %select_convert_fusion.1 = bf16[2560,3072]{1,0:T(8,128)(2,1)} fusion(bf16[2560,3072]{1,0:T(8,128)(2,1)} %maximum_convert_fusion.1, bf16[1,3072,768]{2,1,0:T(8,128)(2,1)} %param.10, bf16[2560,768]{1,0:T(8,128)(2,1)} %get-tuple-element.31, f32[2560]{0:T(1024)S(1)} %get-tuple-element.81, pred[2560]{0:T(1024)(128)(4,1)S(1)} %lt.103), kind=kOutput, calls=%fused_computation.6 | convolution fusion | flops 12111052800 | bytes 40120832 | tf_op jit(solution)/shard_map/nd,fd->nf/dot_general | solution.py:220
  354.3 17.6 %fusion.97 = f32[768,3072]{1,0:T(8,128)} fusion(bf16[2560,768]{1,0:T(8,128)(2,1)S(1)} %copy-done.1, bf16[2560,3072]{1,0:T(8,128)(2,1)} %select_convert_fusion.1), kind=kOutput, calls=%fused_computation.160 | convolution fusion | flops 12079595520 | bytes 29097984 | tf_op jit(solution)/shard_map/nd,nf->df/dot_general | solution.py:231
  372.0 16.0 %convolution_convert_fusion.1 = bf16[2560,768]{1,0:T(8,128)(2,1)} fusion(bf16[2560,3072]{1,0:T(8,128)(2,1)S(1)} %copy-done.11, bf16[1,768,3072]{2,1,0:T(8,128)(2,1)} %param.9), kind=kOutput, calls=%fused_computation.29 | convolution fusion | flops 12081561600 | bytes 24379392 | tf_op jit(solution)/shard_map/nf,df->nd/dot_general | solution.py:222
  388.0 2.9 fusion.47
  390.9 18.7 %maximum_convert_fusion = bf16[2560,3072]{1,0:T(8,128)(2,1)} fusion(bf16[2560,768]{1,0:T(8,128)(2,1)} %bitcast.8, bf16[1,768,3072]{2,1,0:T(8,128)(2,1)} %param.9), kind=kOutput, calls=%fused_computation.7 | convolution fusion | flops 12095324160 | bytes 24379392 | tf_op jit(solution)/shard_map/dot_general | solution.py:208
  409.7 7.4 %all-to-all-done.1 = bf16[32,80,768]{2,1,0:T(8,128)(2,1)} async-done(((bf16[32,80,768]{2,1,0:T(8,128)(2,1)}), bf16[32,80,768]{2,1,0:T(8,128)(2,1)}, u32[]{:S(2)}, u32[]{:S(2)}) %all-to-all-start.1) | async-done | bytes 3932192 | tf_op jit(solution)/shard_map/all_to_all | solution.py:180
  417.1 5.1 all-to-all-start.2
  422.1 17.9 %fusion.9 = f32[2560]{0:T(1024)S(1)} fusion(bf16[32,80,768]{2,1,0:T(8,128)(2,1)} %all-to-all-done.1, bf16[2560,3072]{1,0:T(8,128)(2,1)} %maximum_convert_fusion, bf16[1,3072,768]{2,1,0:T(8,128)(2,1)} %param.10), kind=kOutput, calls=%fused_computation.24 | convolution fusion | flops 12089423872 | bytes 24389632 | tf_op jit(solution)/shard_map/dot_general | solution.py:209
  440.1 2.9 convolution_add_fusion
  443.1 4.0 fusion.29
  447.1 0.2 copy.49
  447.2 0.1 reshape.260
  447.5 0.6 broadcast_in_dim.58
  448.1 0.1 concatenate.7
  448.3 4.0 fusion.8
  452.3 21.4 %select_convert_fusion = bf16[2560,3072]{1,0:T(8,128)(2,1)} fusion(bf16[2560,3072]{1,0:T(8,128)(2,1)} %maximum_convert_fusion, bf16[2560,768]{1,0:T(8,128)(2,1)} %bitcast.101, bf16[1,3072,768]{2,1,0:T(8,128)(2,1)} %param.10), kind=kOutput, calls=%fused_computation.5 | convolution fusion | flops 12103188480 | bytes 40108032 | tf_op jit(solution)/shard_map/nd,fd->nf/dot_general | solution.py:220
  473.6 17.8 %convolution_convert_fusion = bf16[2560,768]{1,0:T(8,128)(2,1)} fusion(bf16[2560,3072]{1,0:T(8,128)(2,1)} %select_convert_fusion, bf16[1,768,3072]{2,1,0:T(8,128)(2,1)} %param.9), kind=kOutput, calls=%fused_computation.28 | convolution fusion | flops 12081561600 | bytes 24379392 | tf_op jit(solution)/shard_map/nf,df->nd/dot_general | solution.py:222
  491.5 17.9 %all-to-all-done.2 = bf16[32,80,768]{2,1,0:T(8,128)(2,1)} async-done(((bf16[32,80,768]{2,1,0:T(8,128)(2,1)}), bf16[32,80,768]{2,1,0:T(8,128)(2,1)}, u32[]{:S(2)}, u32[]{:S(2)}) %all-to-all-start.2) | async-done | bytes 3932192 | tf_op jit(solution)/shard_map/all_to_all | solution.py:180
  509.3 0.8 copy.51
  510.1 5.0 all-to-all-start.3
  515.2 4.5 fusion.11
  519.7 2.3 all-to-all-done.3
  522.1 0.1 slice_reduce_fusion.1
  522.2 1.6 fusion.27
  523.9 5.3 all-to-all-start.4
  529.2 20.0 %fusion.87 = f32[3072,768]{1,0:T(8,128)} fusion(bf16[2560,3072]{1,0:T(8,128)(2,1)} %maximum_convert_fusion.1, bf16[2560,768]{1,0:T(8,128)(2,1)} %get-tuple-element.31, f32[2560]{0:T(1024)S(1)} %get-tuple-element.81, pred[2560]{0:T(1024)(128)(4,1)S(1)} %lt.103), kind=kOutput, calls=%fused_computation.154 | convolution fusion | flops 12087459840 | bytes 29110784 | tf_op jit(solution)/shard_map/nf,nd->fd/dot_general | solution.py:254
  549.2 18.7 %add_bitcast_fusion.1 = f32[1,768,3072]{2,1,0:T(8,128)} fusion(f32[768,3072]{1,0:T(8,128)S(1)} %bitcast.123, bf16[2560,768]{1,0:T(8,128)(2,1)} %bitcast.8, bf16[2560,3072]{1,0:T(8,128)(2,1)} %select_convert_fusion), kind=kOutput, calls=%fused_computation.15 | convolution fusion | flops 12081954816 | bytes 38535168 | tf_op jit(solution)/shard_map/nd,nf->df/dot_general | solution.py:226
  567.9 1.9 fusion.33
  569.8 20.7 %add_bitcast_fusion = f32[1,3072,768]{2,1,0:T(8,128)} fusion(f32[3072,768]{1,0:T(8,128)} %fusion.87, bf16[2560,3072]{1,0:T(8,128)(2,1)} %maximum_convert_fusion, bf16[2560,768]{1,0:T(8,128)(2,1)} %fusion.11), kind=kOutput, calls=%fused_computation.14 | convolution fusion | flops 12081954816 | bytes 38535168 | tf_op jit(solution)/shard_map/nf,nd->fd/dot_general | solution.py:227
  590.6 23.2 %fusion.12 = f32[4096,768]{1,0:T(8,128)} fusion(f32[4096,768]{1,0:T(8,128)S(1)} %fusion.33, bf16[2560,768]{1,0:T(8,128)(2,1)} %bitcast.17, s32[4096]{0:T(1024)S(1)} %copy-done.8), kind=kOutput, calls=%fused_computation.27 | convolution fusion | flops 16119758848 | bytes 29114368 | tf_op jit(solution)/shard_map/dot_general | solution.py:263
  613.8 2.5 all-to-all-done.4
  616.4 0.7 broadcast_in_dim.113
  617.1 5.0 all-to-all-start.5
  622.1 22.8 %add_convert_fusion = bf16[4096,768]{1,0:T(8,128)(2,1)} fusion(f32[4096,768]{1,0:T(8,128)} %fusion.12, bf16[2560,768]{1,0:T(8,128)(2,1)} %bitcast.18, s32[4096]{0:T(1024)S(1)} %copy-done.7), kind=kOutput, calls=%fused_computation.11 | convolution fusion | flops 16122904576 | bytes 22822912 | tf_op jit(solution)/shard_map/dot_general | solution.py:263
  644.8 0.1 fusion.83
  645.0 0.7 slice.61
  645.6 0.1 reshape.265
  645.8 0.8 copy.52
  646.6 0.6 multiply_reduce_fusion.6
  (75 shorter events, 1.5 us)
Async XLA Ops:
  0.6 287.5 %copy-start = (f32[768,32]{0,1:T(8,128)S(1)}, f32[768,32]{0,1:T(8,128)}, u32[]{:S(2)}) copy-start(f32[768,32]{0,1:T(8,128)} %param.7) | copy-start | bytes 294916
  2.5 295.7 %copy-start.5 = (s32[2,2,8,128]{3,1,2,0:T(2,128)}, s32[2,2,8,128]{3,1,2,0:T(2,128)S(1)}, u32[]{:S(2)}) copy-start(s32[2,2,8,128]{3,1,2,0:T(2,128)S(1)} %copy.60) | copy-start | bytes 49156
  185.4 139.1 %all-to-all-start = ((bf16[32,80,768]{2,1,0:T(8,128)(2,1)}), bf16[32,80,768]{2,1,0:T(8,128)(2,1)}, u32[]{:S(2)}, u32[]{:S(2)}) async-start(bf16[32,80,768]{2,1,0:T(8,128)(2,1)} %bitcast.102), calls=%async_computation | async-start | bytes 7864320 | tf_op jit(solution)/shard_map/all_to_all | solution.py:180
  238.5 54.5 %copy-start.9 = (s32[32]{0:T(128)}, s32[32]{0:T(128)S(1)}, u32[]{:S(2)}) copy-start(s32[32]{0:T(128)S(1)} %get-tuple-element.83) | copy-start | bytes 388
  238.6 33.0 %slice-start = ((s8[4718592]{0:T(1024)(128)(4,1)}), s8[524288]{0:T(1024)(128)(4,1)S(1)}, s32[]{:S(2)}) async-start(s8[4718592]{0:T(1024)(128)(4,1)} %bitcast.120), calls=%async_computation.6 | async-start | bytes 1048576
  252.7 18.9 %slice-start.1 = ((s8[4718592]{0:T(1024)(128)(4,1)}), s8[4194304]{0:T(1024)(128)(4,1)S(1)}, s32[]{:S(2)}) async-start(s8[4718592]{0:T(1024)(128)(4,1)} %bitcast.120), calls=%async_computation.7 | async-start | bytes 8388608
  252.7 18.9 %copy-start.12 = (bf16[2560,768]{1,0:T(8,128)(2,1)S(1)}, bf16[2560,768]{1,0:T(8,128)(2,1)}, u32[]{:S(2)}) copy-start(bf16[2560,768]{1,0:T(8,128)(2,1)} %get-tuple-element.31) | copy-start | bytes 11796484
  287.8 5.2 copy-start.2
  324.5 92.5 %all-to-all-start.1 = ((bf16[32,80,768]{2,1,0:T(8,128)(2,1)}), bf16[32,80,768]{2,1,0:T(8,128)(2,1)}, u32[]{:S(2)}, u32[]{:S(2)}) async-start(bf16[32,80,768]{2,1,0:T(8,128)(2,1)} %bitcast.100), calls=%async_computation.1 | async-start | bytes 7864320 | tf_op jit(solution)/shard_map/all_to_all | solution.py:180
  333.6 20.7 %copy-start.1 = (bf16[2560,768]{1,0:T(8,128)(2,1)S(1)}, bf16[2560,768]{1,0:T(8,128)(2,1)}, u32[]{:S(2)}) copy-start(bf16[2560,768]{1,0:T(8,128)(2,1)} %get-tuple-element.30) | copy-start | bytes 11796484
  354.3 17.6 %copy-start.11 = (bf16[2560,3072]{1,0:T(8,128)(2,1)S(1)}, bf16[2560,3072]{1,0:T(8,128)(2,1)}, u32[]{:S(2)}) copy-start(bf16[2560,3072]{1,0:T(8,128)(2,1)} %select_convert_fusion.1) | copy-start | bytes 47185924
  417.1 92.3 %all-to-all-start.2 = ((bf16[32,80,768]{2,1,0:T(8,128)(2,1)}), bf16[32,80,768]{2,1,0:T(8,128)(2,1)}, u32[]{:S(2)}, u32[]{:S(2)}) async-start(bf16[32,80,768]{2,1,0:T(8,128)(2,1)} %bitcast.103), calls=%async_computation.2 | async-start | bytes 7864320 | tf_op jit(solution)/shard_map/all_to_all | solution.py:180
  491.5 30.8 %copy-start.3 = (s32[4096]{0:T(1024)S(1)}, s32[4096]{0:T(1024)}, u32[]{:S(2)}) copy-start(s32[4096]{0:T(1024)} %param.8) | copy-start | bytes 49156
  491.5 30.8 %copy-start.6 = (s32[2,2,8,128]{3,1,2,0:T(2,128)S(1)}, s32[2,2,8,128]{3,1,2,0:T(2,128)}, u32[]{:S(2)}) copy-start(s32[2,2,8,128]{3,1,2,0:T(2,128)} %copy-done.5) | copy-start | bytes 49156
  510.1 11.9 %all-to-all-start.3 = ((f32[32,1,930]{2,1,0:T(1,128)}), f32[32,1,930]{2,1,0:T(1,128)S(1)}, u32[]{:S(2)}, u32[]{:S(2)}) async-start(f32[32,1,930]{2,1,0:T(1,128)} %copy.51), calls=%async_computation.3 | async-start | bytes 262144 | tf_op jit(solution)/shard_map/all_to_all | solution.py:180
  523.9 25.3 %slice-start.2 = ((s8[9437184]{0:T(1024)(128)(4,1)}), s8[1048576]{0:T(1024)(128)(4,1)S(1)}, s32[]{:S(2)}) async-start(s8[9437184]{0:T(1024)(128)(4,1)} %bitcast.122), calls=%async_computation.8 | async-start | bytes 2097152
  523.9 92.5 %all-to-all-start.4 = ((bf16[32,80,768]{2,1,0:T(8,128)(2,1)}), bf16[32,80,768]{2,1,0:T(8,128)(2,1)}, u32[]{:S(2)}, u32[]{:S(2)}) async-start(bf16[32,80,768]{2,1,0:T(8,128)(2,1)} %bitcast.104), calls=%async_computation.4 | async-start | bytes 7864320 | tf_op jit(solution)/shard_map/all_to_all | solution.py:180
  529.1 20.0 %copy-start.4 = (f32[4096]{0:T(1024)S(1)}, f32[4096]{0:T(1024)}, u32[]{:S(2)}) copy-start(f32[4096]{0:T(1024)} %get-tuple-element.77) | copy-start | bytes 49156
  529.2 20.0 %slice-start.3 = ((s8[9437184]{0:T(1024)(128)(4,1)}), s8[4194304]{0:T(1024)(128)(4,1)S(1)}, s32[]{:S(2)}) async-start(s8[9437184]{0:T(1024)(128)(4,1)} %bitcast.122), calls=%async_computation.9 | async-start | bytes 8388608
  529.2 20.0 %slice-start.4 = ((s8[9437184]{0:T(1024)(128)(4,1)}), s8[4194304]{0:T(1024)(128)(4,1)S(1)}, s32[]{:S(2)}) async-start(s8[9437184]{0:T(1024)(128)(4,1)} %bitcast.122), calls=%async_computation.10 | async-start | bytes 8388608
  569.8 20.8 %copy-start.8 = (s32[4096]{0:T(1024)S(1)}, s32[4096]{0:T(1024)}, u32[]{:S(2)}) copy-start(s32[4096]{0:T(1024)} %get-tuple-element.87) | copy-start | bytes 49156
  590.6 31.5 %copy-start.7 = (s32[4096]{0:T(1024)S(1)}, s32[4096]{0:T(1024)}, u32[]{:S(2)}) copy-start(s32[4096]{0:T(1024)} %get-tuple-element.86) | copy-start | bytes 49156
  617.1 27.8 %all-to-all-start.5 = ((f32[32,1,770]{2,1,0:T(1,128)}), f32[32,1,770]{2,1,0:T(1,128)S(1)}, u32[]{:S(2)}, u32[]{:S(2)}) async-start(f32[32,1,770]{2,1,0:T(1,128)} %broadcast_in_dim.113), calls=%async_computation.5 | async-start | bytes 229376 | tf_op jit(solution)/shard_map/all_to_all | solution.py:180
  622.0 24.5 %copy-start.10 = (s32[32]{0:T(128)S(1)}, s32[32]{0:T(128)}, u32[]{:S(2)}) copy-start(s32[32]{0:T(128)} %copy-done.9) | copy-start | bytes 388
